TPU v7x, 32 devices: a 4x2x2 block of a 4x4x8 slice. The times are simulated.
32 devices in a mesh: dp: 4 (over y, z), ep: 8 (over x, core).
Axes of the slice: x: 4, y: 2, z: 2, core: 2. Of those that a mesh axis runs over, the one named last changes fastest.
The devices are a block of a 4x4x8 slice.
Arguments:
- x_in: bfloat16 [8192, 1024], P(('dp', 'ep')), parts along dimension 0
- k_cache: bfloat16 [8192, 32, 8, 64], P(('dp', 'ep')), parts along dimension 0
- v_cache: bfloat16 [8192, 32, 8, 64], P(('dp', 'ep')), parts along dimension 0
- cache_len: int32 [8192], P(('dp', 'ep')), parts along dimension 0
- topk_idx: int32 [8192, 8], P(('dp', 'ep')), parts along dimension 0
- ln_attn: bfloat16 [1024], replicated
- w_q: bfloat16 [1024, 1024], replicated
- w_k: bfloat16 [1024, 512], replicated
- w_v: bfloat16 [1024, 512], replicated
- q_norm: bfloat16 [64], replicated
- k_norm: bfloat16 [64], replicated
- w_o: bfloat16 [1024, 1024], replicated
- ln_moe: bfloat16 [1024], replicated
- w_router: bfloat16 [1024, 32], replicated
- w_gate: bfloat16 [32, 1024, 512], P('ep')
- w_up: bfloat16 [32, 1024, 512], P('ep')
- w_down: bfloat16 [32, 512, 1024], P('ep')
Outputs:
- output 1: bfloat16 [8192, 1024], P(('dp', 'ep')), parts along dimension 0
- output 2: bfloat16 [8192, 32, 8, 64], P(('dp', 'ep')), parts along dimension 0
- output 3: bfloat16 [8192, 32, 8, 64], P(('dp', 'ep')), parts along dimension 0
There are 4 independent parts. A program takes and returns all parts, laid end to end along the dimension named above; an argument that names none is the same for every part.
All inputs are finite; a program needn't handle non-finite values.
Results may differ from a plain program's by a relative error of at most 0.0140908.
Values are sent between devices in bfloat16 or wider.
A program may use at most 768 MiB of HBM per device.

v0:
```python
import jax
import jax.numpy as jnp
from jax import lax
from jax.sharding import PartitionSpec as P

ROPE_BASE = 1000000.0
NORM_EPS = 1e-6


def norm_scale(values, gain_vec):
    return values * lax.rsqrt(jnp.mean(values * values, axis=-1, keepdims=True) + NORM_EPS) * gain_vec.astype(jnp.float32)


def rotate_halves(values, positions):
    half_dim = values.shape[-1] // 2
    freq_vec = ROPE_BASE ** (-jnp.arange(half_dim, dtype=jnp.float32) * 2.0 / values.shape[-1])
    angles = positions.astype(jnp.float32)[:, None, None] * freq_vec
    cosine = jnp.cos(angles)
    sine_val = jnp.sin(angles)
    lo_half = values[..., :half_dim]
    hi_half = values[..., half_dim:]
    return jnp.concatenate([lo_half * cosine - hi_half * sine_val, hi_half * cosine + lo_half * sine_val], axis=-1)


def attend_block(x_in, k_cache, v_cache, cache_len, ln_attn, w_q, w_k, w_v, q_norm, k_norm, w_o):
    n_batch, n_slots, kv_heads, head_dim = k_cache.shape
    q_heads = w_q.shape[1] // head_dim
    resid_in = x_in.astype(jnp.float32)
    normed = norm_scale(resid_in, ln_attn).astype(jnp.bfloat16)
    q_proj = jnp.dot(normed, w_q, preferred_element_type=jnp.float32).reshape(n_batch, q_heads, head_dim)
    k_proj = jnp.dot(normed, w_k, preferred_element_type=jnp.float32).reshape(n_batch, kv_heads, head_dim)
    v_new = jnp.dot(normed, w_v, preferred_element_type=jnp.float32).astype(jnp.bfloat16).reshape(n_batch, kv_heads, head_dim)
    q_rot = rotate_halves(norm_scale(q_proj, q_norm), cache_len).astype(jnp.bfloat16).reshape(n_batch, kv_heads, q_heads // kv_heads, head_dim)
    k_new = rotate_halves(norm_scale(k_proj, k_norm), cache_len).astype(jnp.bfloat16)
    len_col = cache_len[:, None, None, None]
    is_new = lax.broadcasted_iota(jnp.int32, (1, n_slots, 1, 1), 1) == len_col
    k_full = jnp.where(is_new, k_new[:, None], k_cache)
    v_full = jnp.where(is_new, v_new[:, None], v_cache)
    scores = jnp.einsum('bgrd,bsgd->bgrs', q_rot, k_full, preferred_element_type=jnp.float32) * head_dim ** -0.5
    seen = lax.broadcasted_iota(jnp.int32, (1, 1, 1, n_slots), 3) <= len_col
    attn_prob = jax.nn.softmax(jnp.where(seen, scores, -1e30), axis=-1).astype(jnp.bfloat16)
    attn_out = jnp.einsum('bgrs,bsgd->bgrd', attn_prob, v_full, preferred_element_type=jnp.float32).astype(jnp.bfloat16).reshape(n_batch, q_heads * head_dim)
    x_mid = (resid_in + jnp.dot(attn_out, w_o, preferred_element_type=jnp.float32)).astype(jnp.bfloat16)
    return x_mid, k_full, v_full


def route_gate(x_mid, ln_moe, w_router, topk_idx):
    resid_mid = x_mid.astype(jnp.float32)
    h_moe = norm_scale(resid_mid, ln_moe).astype(jnp.bfloat16)
    logits = jnp.dot(h_moe, w_router, preferred_element_type=jnp.float32)
    gate_wts = jax.nn.softmax(jnp.take_along_axis(logits, topk_idx, axis=1), axis=-1)
    return resid_mid, h_moe, gate_wts


def pack_rows(h_moe, topk_idx, ep_size, e_local, cap_rows):
    b_dev, top_k = topk_idx.shape
    pair_count = b_dev * top_k
    flat_idx = topk_idx.reshape(pair_count)
    dest_dev = flat_idx // e_local
    dest_hot = (dest_dev[:, None] == jnp.arange(ep_size)[None, :]).astype(jnp.int32)
    dev_counts = jnp.sum(dest_hot, axis=0)
    slot_rank = jnp.sum(jnp.cumsum(dest_hot, axis=0) * dest_hot, axis=1) - 1
    dev_start = jnp.cumsum(dev_counts) - dev_counts
    sort_order = jnp.argsort(dest_dev, stable=True)
    seat_ids = jnp.arange(cap_rows)
    pair_at = sort_order[jnp.minimum(dev_start[:, None] + seat_ids[None, :], pair_count - 1)]
    filled = seat_ids[None, :] < dev_counts[:, None]
    send_rows = jnp.where(filled[:, :, None], h_moe[pair_at // top_k], jnp.zeros((), jnp.bfloat16))
    send_ids = jnp.where(filled, (flat_idx % e_local)[pair_at], e_local - 1)
    return send_rows, send_ids, dest_dev * cap_rows + slot_rank


def group_count(row_ids, e_local):
    return jnp.sum((row_ids[:, None] == jnp.arange(e_local)[None, :]).astype(jnp.int32), axis=0)


def expert_sorted(sorted_rows, group_sizes, w_gate, w_up, w_down):
    gate_act = lax.ragged_dot(sorted_rows, w_gate, group_sizes, preferred_element_type=jnp.float32)
    up_act = lax.ragged_dot(sorted_rows, w_up, group_sizes, preferred_element_type=jnp.float32)
    hidden_act = (jax.nn.silu(gate_act) * up_act).astype(jnp.bfloat16)
    return lax.ragged_dot(hidden_act, w_down, group_sizes, preferred_element_type=jnp.float32).astype(jnp.bfloat16)


def expert_rows(tok_rows, row_ids, w_gate, w_up, w_down):
    sort_order = jnp.argsort(row_ids, stable=True)
    sorted_out = expert_sorted(tok_rows[sort_order], group_count(row_ids, w_gate.shape[0]), w_gate, w_up, w_down)
    return sorted_out[jnp.argsort(sort_order, stable=True)]


def unpack_rows(back_rows, flat_slot, gate_wts):
    b_dev, top_k = gate_wts.shape
    picked = back_rows[flat_slot].reshape(b_dev, top_k, back_rows.shape[1])
    return jnp.sum(picked.astype(jnp.float32) * gate_wts[:, :, None], axis=1)


def solution(mesh):
    ep_size = mesh.shape['ep']
    row_spec = P(('dp', 'ep'))
    replicated = P()
    expert_spec = P('ep')
    in_specs = (row_spec, row_spec, row_spec, row_spec, row_spec, replicated, replicated, replicated, replicated, replicated, replicated, replicated, replicated, replicated, expert_spec, expert_spec, expert_spec)
    out_specs = (row_spec, row_spec, row_spec)

    def device_step(x_in, k_cache, v_cache, cache_len, topk_idx, ln_attn, w_q, w_k, w_v, q_norm, k_norm, w_o, ln_moe, w_router, w_gate, w_up, w_down):
        x_mid, k_full, v_full = attend_block(x_in, k_cache, v_cache, cache_len, ln_attn, w_q, w_k, w_v, q_norm, k_norm, w_o)
        resid_mid, h_moe, gate_wts = route_gate(x_mid, ln_moe, w_router, topk_idx)
        b_dev, top_k = topk_idx.shape
        hidden = h_moe.shape[1]
        e_local = w_gate.shape[0]
        cap_rows = min(b_dev, 2 * b_dev * top_k // ep_size)
        send_rows, send_ids, flat_slot = pack_rows(h_moe, topk_idx, ep_size, e_local, cap_rows)
        recv_rows = lax.all_to_all(send_rows, 'ep', 0, 0, tiled=True).reshape(ep_size * cap_rows, hidden)
        recv_ids = lax.all_to_all(send_ids, 'ep', 0, 0, tiled=True).reshape(ep_size * cap_rows)
        expert_out = expert_rows(recv_rows, recv_ids, w_gate, w_up, w_down)
        back_rows = lax.all_to_all(expert_out.reshape(ep_size, cap_rows, hidden), 'ep', 0, 0, tiled=True).reshape(ep_size * cap_rows, hidden)
        moe_out = unpack_rows(back_rows, flat_slot, gate_wts)
        return (resid_mid + moe_out).astype(jnp.bfloat16), k_full, v_full

    return jax.shard_map(device_step, mesh=mesh, in_specs=in_specs, out_specs=out_specs, check_vma=False)
```

profile of v0, /device:TPU:81, one launch (start us, length us, event | category | flops | bytes accessed | tf_op | source)
XLA Modules:
  0.0 363.0 jit_solution(13512519605898381938)
XLA Ops:
  5.7 5.0 %sort.45 = (s32[2048]{0:T(1024)}, s32[2048]{0:T(1024)S(1)}) sort(s32[2048]{0:T(1024)S(1)} %get-tuple-element.31, s32[2048]{0:T(1024)S(1)} %iota.60), dimensions={0}, to_apply=%region_7.8 | sort | flops 22528 | bytes 32768 | tf_op jit(solution)/shard_map/jit(argsort)/sort | solution.py:64
  10.7 11.8 %gather_fusion = s32[2048]{0:T(1024)S(1)} fusion(s32[2048]{0:T(1024)S(1)} %get-tuple-element.6, s32[2048]{0:T(1024)S(1)} %broadcast_clamp_fusion.2), kind=kCustom, calls=%fused_computation | custom fusion | bytes 24576 | tf_op jit(solution)/shard_map/gather | solution.py:66
  22.6 11.8 %gather_fusion.2 = s32[2048]{0:T(1024)S(1)} fusion(s32[2048]{0:T(1024)S(1)} %get-tuple-element.32, s32[2048]{0:T(1024)S(1)} %broadcast_clamp_fusion.3), kind=kCustom, calls=%fused_computation.2 | custom fusion | bytes 24576 | tf_op jit(solution)/shard_map/gather | solution.py:69
  35.1 6.0 %all-to-all-start.1 = ((s32[8,1,256]{2,1,0:T(1,128)}), s32[8,1,256]{2,1,0:T(1,128)S(1)}, u32[]{:S(2)}, u32[]{:S(2)}) async-start(s32[8,1,256]{2,1,0:T(1,128)} %compare_select_fusion.1), calls=%async_computation.1 | async-start | bytes 16384 | tf_op jit(solution)/shard_map/all_to_all | solution.py:113
  48.7 11.7 %broadcast_select_fusion.1 = (bf16[256,32,8,64]{0,3,2,1:T(8,128)(2,1)}, bf16[256,32,8,64]{0,3,2,1:T(8,128)(2,1)}) fusion(bf16[256,32,8,64]{0,3,2,1:T(8,128)(2,1)} %param.18, pred[256,32]{0,1:T(8,128)(4,1)S(1)} %copy.63, bf16[256,8,64]{0,2,1:T(8,128)(2,1)S(1)} %pad_maximum_fusion, bf16[256,32,8,64]{0,3,2,1:T(8,128)(2,1)} %param.19, ...), kind=kLoop, calls=%fused_computation.11 | loop fusion | flops 8388608 | bytes 34086912 | tf_op jit(solution)/shard_map/jit(_where)/select_n | solution.py:37
  60.3 24.1 %copy.65 = bf16[256,32,8,64]{3,1,2,0:T(8,128)(2,1)} copy(bf16[256,32,8,64]{0,3,2,1:T(8,128)(2,1)} %get-tuple-element.29) | data formatting | bytes 16777216 | tf_op jit(solution)/shard_map/jit(_where)/select_n | solution.py:37
  87.8 24.0 %copy.67 = bf16[256,32,8,64]{3,1,2,0:T(8,128)(2,1)} copy(bf16[256,32,8,64]{0,3,2,1:T(8,128)(2,1)} %get-tuple-element.30) | data formatting | bytes 16777216 | tf_op jit(solution)/shard_map/jit(_where)/select_n | solution.py:38
  111.8 15.4 %fusion.37 = (f32[256,8,2]{2,1,0:T(8,128)}, f32[256,8,2,32]{3,2,1,0:T(2,128)}) fusion(pred[256,32]{1,0:T(8,128)(4,1)S(1)} %copy-done.7, bf16[256,32,8,64]{3,1,2,0:T(8,128)(2,1)} %copy.65, bf16[256,8,2,32]{3,2,1,0:T(2,128)(2,1)S(1)} %bitcast.69, bf16[256,8,2,32]{3,2,1,0:T(2,128)(2,1)S(1)} %bitcast.68), kind=kOutput, calls=%fused_computation.121 | convolution fusion | flops 18350112 | bytes 9461760 | tf_op jit(solution)/shard_map/sub | solution.py:41
  127.2 10.0 %convolution_convert_fusion = bf16[256,8,2,64]{3,2,1,0:T(2,128)(2,1)} fusion(bf16[256,32,8,64]{3,1,2,0:T(8,128)(2,1)} %copy.67, f32[256,8,2,32]{3,2,1,0:T(2,128)} %get-tuple-element.42, f32[256,8,2]{2,1,0:T(8,128)} %get-tuple-element.41), kind=kOutput, calls=%fused_computation.23 | convolution fusion | flops 17301504 | bytes 9453568 | tf_op jit(solution)/shard_map/bgrs,bsgd->bgrd/dot_general | solution.py:42
  141.8 9.7 %gather_fusion.1 = bf16[2048,1024]{1,0:T(8,128)(2,1)} fusion(bf16[256,1024]{1,0:T(8,128)(2,1)S(1)} %fusion.8, s32[2048]{0:T(1024)S(1)} %broadcast_clamp_fusion), kind=kCustom, calls=%fused_computation.1 | custom fusion | bytes 8396800 | tf_op jit(solution)/shard_map/gather | solution.py:68
  160.1 5.0 %sort.46 = (s32[2048]{0:T(1024)}, s32[2048]{0:T(1024)S(1)}) sort(s32[2048]{0:T(1024)S(1)} %bitcast.70, s32[2048]{0:T(1024)S(1)} %iota.61), dimensions={0}, to_apply=%region_9.10 | sort | flops 22528 | bytes 32768 | tf_op jit(solution)/shard_map/jit(argsort)/sort | solution.py:85
  167.2 5.0 %sort.47 = (s32[2048]{0:T(1024)}, s32[2048]{0:T(1024)S(1)}) sort(s32[2048]{0:T(1024)S(1)} %get-tuple-element.7, s32[2048]{0:T(1024)S(1)} %iota.62), dimensions={0}, to_apply=%region_11.12 | sort | flops 22528 | bytes 32768 | tf_op jit(solution)/shard_map/jit(argsort)/sort | solution.py:87
  172.2 36.4 %all-to-all-done = bf16[8,256,1024]{2,1,0:T(8,128)(2,1)} async-done(((bf16[8,256,1024]{2,1,0:T(8,128)(2,1)}), bf16[8,256,1024]{2,1,0:T(8,128)(2,1)}, u32[]{:S(2)}, u32[]{:S(2)}) %all-to-all-start) | async-done | bytes 4194336 | tf_op jit(solution)/shard_map/all_to_all | solution.py:112
  208.6 13.9 %gather_fusion.3 = bf16[2048,1024]{1,0:T(8,128)(2,1)} fusion(bf16[2048,1024]{1,0:T(8,128)(2,1)} %bitcast.11, s32[2048]{0:T(1024)S(1)} %fusion.22), kind=kCustom, calls=%fused_computation.3 | custom fusion | bytes 8396800 | tf_op jit(solution)/shard_map/gather | solution.py:86
  222.6 13.5 %ragged-dot-none.2 = f32[2048,512]{1,0:T(8,128)} custom-call(s32[1]{0:T(128)} %get-tuple-element.9, s32[5]{0:T(128)} %get-tuple-element.10, s32[11]{0:T(128)} %get-tuple-element.11, s32[11]{0:T(128)} %get-tuple-element.12, s32[1]{0:T(128)} %get-tuple-element.9, bf16[2048,1024]{1,0:T(8,128)(2,1)} %gather_fusion.3, bf16[4,1024,512]{2,1,0:T(8,128)(2,1)} %param.31), custom_call_target="tpu_custom_call" | custom-call | flops 2147483648 | bytes 12582928 | tf_op jit(solution)/shard_map/ragged_dot_general/ragged-dot-none
  236.1 13.5 %ragged-dot-none.1 = f32[2048,512]{1,0:T(8,128)} custom-call(s32[1]{0:T(128)} %get-tuple-element.9, s32[5]{0:T(128)} %get-tuple-element.10, s32[11]{0:T(128)} %get-tuple-element.11, s32[11]{0:T(128)} %get-tuple-element.12, s32[1]{0:T(128)} %get-tuple-element.9, bf16[2048,1024]{1,0:T(8,128)(2,1)} %gather_fusion.3, bf16[4,1024,512]{2,1,0:T(8,128)(2,1)} %param.32), custom_call_target="tpu_custom_call" | custom-call | flops 2147483648 | bytes 12582928 | tf_op jit(solution)/shard_map/ragged_dot_general/ragged-dot-none
  249.5 6.2 %multiply_convert_fusion = bf16[2048,512]{1,0:T(8,128)(2,1)} fusion(f32[2048,512]{1,0:T(8,128)} %ragged-dot-none.1, f32[2048,512]{1,0:T(8,128)} %ragged-dot-none.2), kind=kLoop, calls=%fused_computation.12 | loop fusion | flops 6291456 | bytes 10485760 | tf_op jit(solution)/shard_map/convert_element_type | solution.py:80
  255.7 13.9 %ragged-dot-none = f32[2048,1024]{1,0:T(8,128)} custom-call(s32[1]{0:T(128)} %get-tuple-element.9, s32[5]{0:T(128)} %get-tuple-element.10, s32[11]{0:T(128)} %get-tuple-element.11, s32[11]{0:T(128)} %get-tuple-element.12, s32[1]{0:T(128)} %get-tuple-element.9, bf16[2048,512]{1,0:T(8,128)(2,1)} %multiply_convert_fusion, bf16[4,512,1024]{2,1,0:T(8,128)(2,1)} %param.33), custom_call_target="tpu_custom_call" | custom-call | flops 2147483648 | bytes 14680080 | tf_op jit(solution)/shard_map/ragged_dot_general/ragged-dot-none
  269.6 6.0 %convert_element_type.88 = bf16[2048,1024]{1,0:T(8,128)(2,1)} convert(f32[2048,1024]{1,0:T(8,128)} %ragged-dot-none) | non-fusion elementwise | flops 2097152 | bytes 12582912 | tf_op jit(solution)/shard_map/convert_element_type | solution.py:81
  275.6 13.7 %gather_fusion.4 = bf16[2048,1024]{1,0:T(8,128)(2,1)} fusion(bf16[2048,1024]{1,0:T(8,128)(2,1)} %convert_element_type.88, s32[2048]{0:T(1024)S(1)} %fusion.23), kind=kCustom, calls=%fused_computation.4 | custom fusion | bytes 8396800 | tf_op jit(solution)/shard_map/gather | solution.py:87
  289.4 5.4 %all-to-all-start.2 = ((bf16[8,256,1024]{2,1,0:T(8,128)(2,1)}), bf16[8,256,1024]{2,1,0:T(8,128)(2,1)}, u32[]{:S(2)}, u32[]{:S(2)}) async-start(bf16[8,256,1024]{2,1,0:T(8,128)(2,1)} %bitcast.65), calls=%async_computation.2 | async-start | bytes 8388608 | tf_op jit(solution)/shard_map/all_to_all | solution.py:115
  295.4 16.8 %gather_fusion.6 = f32[2048]{0:T(1024)S(1)} fusion(f32[256,32]{0,1:T(8,128)S(1)} %fusion.40, s32[2048]{0:T(1024)S(1)} %reshape.610), kind=kCustom, calls=%fused_computation.6 | custom fusion | bytes 32768 | tf_op jit(solution)/shard_map/jit(take_along_axis)/gather | solution.py:51
  312.6 30.7 %all-to-all-done.2 = bf16[8,256,1024]{2,1,0:T(8,128)(2,1)} async-done(((bf16[8,256,1024]{2,1,0:T(8,128)(2,1)}), bf16[8,256,1024]{2,1,0:T(8,128)(2,1)}, u32[]{:S(2)}, u32[]{:S(2)}) %all-to-all-start.2) | async-done | bytes 4194336 | tf_op jit(solution)/shard_map/all_to_all | solution.py:115
  343.4 13.9 %gather_fusion.5 = bf16[2048,1024]{1,0:T(8,128)(2,1)} fusion(bf16[2048,1024]{1,0:T(8,128)(2,1)} %bitcast.13, s32[2048]{0:T(1024)S(1)} %broadcast_clamp_fusion.1), kind=kCustom, calls=%fused_computation.5 | custom fusion | bytes 8396800 | tf_op jit(solution)/shard_map/gather | solution.py:92
  (106 shorter events, 38.5 us)
Async XLA Ops:
  0.6 83.8 %copy-start = (bf16[1024,1024]{1,0:T(8,128)(2,1)S(1)}, bf16[1024,1024]{1,0:T(8,128)(2,1)}, u32[]{:S(2)}) copy-start(bf16[1024,1024]{1,0:T(8,128)(2,1)} %param.23) | copy-start | bytes 6291460
  22.5 18.5 %copy-start.9 = (s32[256]{0:T(256)S(1)}, s32[256]{0:T(256)}, u32[]{:S(2)}) copy-start(s32[256]{0:T(256)} %param.20) | copy-start | bytes 3076
  22.6 19.9 %copy-start.10 = (bf16[1024]{0:T(1024)(128)(2,1)S(1)}, bf16[1024]{0:T(1024)(128)(2,1)}, u32[]{:S(2)}) copy-start(bf16[1024]{0:T(1024)(128)(2,1)} %param.22) | copy-start | bytes 6148
  22.6 19.9 %copy-start.3 = (bf16[256,1024]{1,0:T(8,128)(2,1)S(1)}, bf16[256,1024]{1,0:T(8,128)(2,1)}, u32[]{:S(2)}) copy-start(bf16[256,1024]{1,0:T(8,128)(2,1)} %param.17) | copy-start | bytes 1572868
  22.6 22.7 %copy-start.12 = (bf16[64]{0:T(256)(128)(2,1)S(1)}, bf16[64]{0:T(256)(128)(2,1)}, u32[]{:S(2)}) copy-start(bf16[64]{0:T(256)(128)(2,1)} %param.27) | copy-start | bytes 388
  35.1 120.2 %all-to-all-start.1 = ((s32[8,1,256]{2,1,0:T(1,128)}), s32[8,1,256]{2,1,0:T(1,128)S(1)}, u32[]{:S(2)}, u32[]{:S(2)}) async-start(s32[8,1,256]{2,1,0:T(1,128)} %compare_select_fusion.1), calls=%async_computation.1 | async-start | bytes 16384 | tf_op jit(solution)/shard_map/all_to_all | solution.py:113
  60.3 25.1 %copy-start.13 = (bf16[64]{0:T(256)(128)(2,1)S(1)}, bf16[64]{0:T(256)(128)(2,1)}, u32[]{:S(2)}) copy-start(bf16[64]{0:T(256)(128)(2,1)} %param.26) | copy-start | bytes 388
  87.8 24.0 %copy-start.7 = (pred[256,32]{1,0:T(8,128)(4,1)S(1)}, pred[256,32]{1,0:T(8,128)(4,1)}, u32[]{:S(2)}) copy-start(pred[256,32]{1,0:T(8,128)(4,1)} %get-tuple-element.35) | copy-start | bytes 24580
  127.2 12.4 %copy-start.2 = (bf16[1024,1024]{1,0:T(8,128)(2,1)S(1)}, bf16[1024,1024]{1,0:T(8,128)(2,1)}, u32[]{:S(2)}) copy-start(bf16[1024,1024]{1,0:T(8,128)(2,1)} %param.28) | copy-start | bytes 6291460
  137.2 4.3 %copy-start.11 = (bf16[1024]{0:T(1024)(128)(2,1)S(1)}, bf16[1024]{0:T(1024)(128)(2,1)}, u32[]{:S(2)}) copy-start(bf16[1024]{0:T(1024)(128)(2,1)} %param.29) | copy-start | bytes 6148
  141.8 9.7 %copy-start.8 = (pred[8,256]{1,0:T(8,128)(4,1)S(1)}, pred[8,256]{1,0:T(8,128)(4,1)}, u32[]{:S(2)}) copy-start(pred[8,256]{1,0:T(8,128)(4,1)} %iota_compare_fusion.5) | copy-start | bytes 6148
  155.2 53.4 %all-to-all-start = ((bf16[8,256,1024]{2,1,0:T(8,128)(2,1)}), bf16[8,256,1024]{2,1,0:T(8,128)(2,1)}, u32[]{:S(2)}, u32[]{:S(2)}) async-start(bf16[8,256,1024]{2,1,0:T(8,128)(2,1)} %broadcast_select_fusion.2), calls=%async_computation | async-start | bytes 8388608 | tf_op jit(solution)/shard_map/all_to_all | solution.py:112
  289.3 5.5 %copy-start.4 = (s32[256,8]{0,1:T(8,128)S(1)}, s32[256,8]{0,1:T(8,128)}, u32[]{:S(2)}) copy-start(s32[256,8]{0,1:T(8,128)} %param.21) | copy-start | bytes 24580
  289.4 5.7 %copy-start.5 = (bf16[1024,32]{0,1:T(8,128)(2,1)S(1)}, bf16[1024,32]{0,1:T(8,128)(2,1)}, u32[]{:S(2)}) copy-start(bf16[1024,32]{0,1:T(8,128)(2,1)} %param.30) | copy-start | bytes 196612
  289.4 54.0 %all-to-all-start.2 = ((bf16[8,256,1024]{2,1,0:T(8,128)(2,1)}), bf16[8,256,1024]{2,1,0:T(8,128)(2,1)}, u32[]{:S(2)}, u32[]{:S(2)}) async-start(bf16[8,256,1024]{2,1,0:T(8,128)(2,1)} %bitcast.65), calls=%async_computation.2 | async-start | bytes 8388608 | tf_op jit(solution)/shard_map/all_to_all | solution.py:115
  295.4 17.2 %copy-start.6 = (s32[2048]{0:T(1024)S(1)}, s32[2048]{0:T(1024)}, u32[]{:S(2)}) copy-start(s32[2048]{0:T(1024)} %get-tuple-element.21) | copy-start | bytes 24580
  343.4 19.6 %copy-start.1 = (bf16[1024,1024]{1,0:T(8,128)(2,1)S(1)}, bf16[1024,1024]{1,0:T(8,128)(2,1)}, u32[]{:S(2)}) copy-start(bf16[1024,1024]{1,0:T(8,128)(2,1)} %param.23) | copy-start | bytes 6291460
where the time goes:
time: 366 us; the launch traced here: 363 us
  local copies, waits for them, and re-layouts  146 us (40%)
  waiting for transfers between devices  67.1 us (18%)
  other arithmetic  57.1 us (16%)
  Pallas kernels  42.3 us (12%)
  matrix products  32.9 us (9%)
  starting transfers between devices  16.2 us (4%)
    another operation x3, Pallas kernels  40.9 us
    all_to_all x1, waiting for transfers between devices, device_step(): lax.all_to_all(send_rows, 'ep', 0, 0, tiled=True)  36.4 us
    all_to_all x1, waiting for transfers between devices, device_step(): lax.all_to_all(expert_out.reshape(ep_size, cap_rows, hidden), 'ep', 0, 0,...  30.7 us
    select_n x1, local copies, waits for them, and re-layouts, attend_block(): k_full = jnp.where(is_new, k_new[:, None], k_cache)  24.1 us
    select_n x1, local copies, waits for them, and re-layouts, attend_block(): v_full = jnp.where(is_new, v_new[:, None], v_cache)  24 us
    gather x5, local copies, waits for them, and re-layouts, route_gate(): jnp.take_along_axis(logits, topk_idx, axis=1)  17.2 us
    sub x1, matrix products, attend_block(): jax.nn.softmax(jnp.where(seen, scores, -1e+30), axis=-1)  15.4 us
    gather x1, local copies, waits for them, and re-layouts, expert_rows(): tok_rows[sort_order]  13.9 us
  transfers between devices with their start and end apart: 3, of which 2 were waited for; matrix products, arithmetic and copies ran while one was open for 39% of the time, Pallas kernels for 0%

commit v1 on v0

v1 whole, which is shorter than its diff:
```python
import functools

import jax
import jax.numpy as jnp
import numpy as np
from jax import lax
from jax.experimental import pallas as pl
from jax.experimental.pallas import tpu as pltpu
from jax.sharding import PartitionSpec as P

ROPE_BASE = 1000000.0
NORM_EPS = 1e-6
F32 = jnp.float32
BF16 = jnp.bfloat16
MESH = pl.DeviceIdType.MESH


def attn_kernel(freq_ref, x_ref, len_ref, topk_ref, lna_ref, qn_ref, kn_ref, wq_ref, wk_ref, wv_ref, wo_hbm, lnm_ref, wr_ref, kc_ref, vc_ref,
                x1_ref, h2_ref, ri_ref, kco_ref, vco_ref,
                h_scr, cos_scr, sin_scr, qg_scr, kg_scr, len_scr, q_scr, kn_scr, vn_scr, s_scr, o_scr, wo_scr, wo_sem):
    step = pl.program_id(0)
    last = pl.num_programs(0) - 1
    n_tok = x_ref.shape[0]
    n_slots, _, head_dim, _ = kc_ref.shape
    half = head_dim // 2
    n_lt = n_tok // 128
    wo_copy = pltpu.make_async_copy(wo_hbm, wo_scr, wo_sem)

    @pl.when(step == 0)
    def _():
        wo_copy.start()
        xf = x_ref[...].astype(F32)
        ms = jnp.mean(xf * xf, axis=1, keepdims=True)
        h_scr[...] = (xf * lax.rsqrt(ms + NORM_EPS) * lna_ref[...].astype(F32)).astype(BF16)
        lens = len_ref[...].astype(F32)
        freq = jnp.concatenate([freq_ref[...]] * n_lt, axis=1)
        angles = freq * lens
        cos_scr[...] = jnp.cos(angles)
        sin_scr[...] = jnp.sin(angles)
        for src, dst in ((qn_ref, qg_scr), (kn_ref, kg_scr)):
            row = src[...].astype(F32)
            wide = jnp.broadcast_to(jnp.concatenate([row, row], axis=1), (128, 128))
            dst[...] = wide.T[:head_dim]
        len_scr[...] = jnp.broadcast_to(lens, (head_dim, n_tok)).astype(BF16)

    def head_rope(block, gain_scr):
        ms = jnp.mean(block * block, axis=0, keepdims=True)
        gain = jnp.concatenate([gain_scr[...]] * n_lt, axis=1)
        block = block * lax.rsqrt(ms + NORM_EPS) * gain
        lo, hi = block[:half], block[half:]
        cosv, sinv = cos_scr[...], sin_scr[...]
        return jnp.concatenate([lo * cosv - hi * sinv, hi * cosv + lo * sinv], axis=0).astype(BF16)

    q_t = jnp.dot(h_scr[...], wq_ref[...], preferred_element_type=F32).T
    for j in range(2):
        q_scr[j] = head_rope(q_t[j * head_dim:(j + 1) * head_dim], qg_scr).astype(F32)

    @pl.when(step % 2 == 0)
    def _():
        k_t = jnp.dot(h_scr[...], wk_ref[...], preferred_element_type=F32).T
        v_t = jnp.dot(h_scr[...], wv_ref[...], preferred_element_type=F32).T
        for j in range(2):
            kn_scr[j] = head_rope(k_t[j * head_dim:(j + 1) * head_dim], kg_scr)
            vn_scr[j] = v_t[j * head_dim:(j + 1) * head_dim].astype(BF16)

    par = step % 2
    for lt in range(n_lt):
        lanes = pl.ds(lt * 128, 128)

        def score_block(i, carry):
            rows = [[], []]
            for si in range(8):
                s = i * 8 + si
                hit = len_scr[:, lanes] == s.astype(F32).astype(BF16)
                kb = jnp.where(hit, kn_scr[par, :, lanes], kc_ref[s, 0, :, lanes])
                kco_ref[s, 0, :, lanes] = kb
                kf = kb.astype(F32)
                for j in range(2):
                    rows[j].append(jnp.sum(kf * q_scr[j, :, lanes], axis=0, keepdims=True))
            for j in range(2):
                s_scr[j, pl.ds(pl.multiple_of(i * 8, 8), 8), lanes] = jnp.concatenate(rows[j], axis=0)
            return carry

        lax.fori_loop(0, n_slots // 8, score_block, 0)
        lens = len_ref[:, lanes]
        seen = lax.broadcasted_iota(jnp.int32, (n_slots, 128), 0) <= lens
        for j in range(2):
            sc = jnp.where(seen, s_scr[j, :, lanes] * (head_dim ** -0.5), -1e30)
            ex = jnp.exp(sc - jnp.max(sc, axis=0, keepdims=True))
            pr = ex / jnp.sum(ex, axis=0, keepdims=True)
            s_scr[j, :, lanes] = pr.astype(BF16).astype(F32)

        def value_block(i, accs):
            accs = list(accs)
            prob = [s_scr[j, pl.ds(pl.multiple_of(i * 8, 8), 8), lanes] for j in range(2)]
            for si in range(8):
                s = i * 8 + si
                hit = len_scr[:, lanes] == s.astype(F32).astype(BF16)
                vb = jnp.where(hit, vn_scr[par, :, lanes], vc_ref[s, 0, :, lanes])
                vco_ref[s, 0, :, lanes] = vb
                vf = vb.astype(F32)
                for j in range(2):
                    accs[j] = accs[j] + prob[j][si:si + 1] * vf
            return tuple(accs)

        zero = jnp.zeros((head_dim, 128), F32)
        accs = lax.fori_loop(0, n_slots // 8, value_block, (zero, zero))
        o_scr[pl.ds(lt * 128, 128), pl.ds(pl.multiple_of(step * 128, 128), 128)] = jnp.concatenate(accs, axis=0).T.astype(BF16)

    @pl.when(step == last)
    def _():
        wo_copy.wait()
        x1 = (x_ref[...].astype(F32) + jnp.dot(o_scr[...], wo_scr[...], preferred_element_type=F32)).astype(BF16)
        x1_ref[...] = x1
        xf = x1.astype(F32)
        ms = jnp.mean(xf * xf, axis=1, keepdims=True)
        h2 = (xf * lax.rsqrt(ms + NORM_EPS) * lnm_ref[...].astype(F32)).astype(BF16)
        h2_ref[...] = h2
        logits = lax.dot_general(wr_ref[...], h2, (((1,), (1,)), ((), ())), preferred_element_type=F32)
        top_k = topk_ref.shape[0]
        n_exp = wr_ref.shape[0]
        n_dev = ri_ref.shape[1]
        e_local = n_exp // n_dev
        exp_id = lax.broadcasted_iota(jnp.int32, (n_exp, n_tok), 0)
        picked = [jnp.sum(jnp.where(exp_id == topk_ref[pl.ds(k, 1), :], logits, 0.0), axis=0, keepdims=True) for k in range(top_k)]
        picked = jnp.concatenate(picked, axis=0)
        ex = jnp.exp(picked - jnp.max(picked, axis=0, keepdims=True))
        gate = ex / jnp.sum(ex, axis=0, keepdims=True)
        dev_id = lax.broadcasted_iota(jnp.int32, (n_dev, n_tok), 0)
        r_dev = jnp.zeros((n_dev, n_tok), F32)
        i_dev = jnp.zeros((n_dev, n_tok), F32)
        for k in range(top_k):
            idx = topk_ref[pl.ds(k, 1), :]
            dev = idx // e_local
            mine = dev_id == dev
            r_dev = r_dev + jnp.where(mine, gate[k:k + 1], 0.0)
            i_dev = i_dev + jnp.where(mine, (idx - dev * e_local).astype(F32), 0.0)
        ri_ref[0] = r_dev
        ri_ref[1] = i_dev


def attention(x_in, k_cache, v_cache, cache_len, topk_idx, ln_attn, w_q, w_k, w_v, q_norm, k_norm, w_o, ln_moe, w_router, ep_size):
    n_tok, hidden = x_in.shape
    _, n_slots, kv_heads, head_dim = k_cache.shape
    freq = np.float32(ROPE_BASE) ** (-np.arange(head_dim // 2, dtype=np.float32) * np.float32(2.0) / np.float32(head_dim))
    freq = jnp.asarray(np.ascontiguousarray(np.broadcast_to(freq[:, None], (head_dim // 2, 128))), F32)
    kt = k_cache.transpose(1, 2, 3, 0)
    vt = v_cache.transpose(1, 2, 3, 0)
    whole = lambda shape: pl.BlockSpec(shape, lambda p: (0,) * len(shape))
    cache_spec = pl.BlockSpec((n_slots, 1, head_dim, n_tok), lambda p: (0, p, 0, 0))
    pair_spec = pl.BlockSpec((hidden, 128), lambda p: (0, p // 2))
    out = pl.pallas_call(
        attn_kernel,
        grid=(kv_heads,),
        in_specs=[
            whole(freq.shape), whole((n_tok, hidden)), whole((1, n_tok)), whole((topk_idx.shape[1], n_tok)), whole((1, hidden)), whole((1, head_dim)), whole((1, head_dim)),
            pl.BlockSpec((hidden, 128), lambda p: (0, p)), pair_spec, pair_spec, pl.BlockSpec(memory_space=pl.ANY), whole((1, hidden)), whole((w_router.shape[1], hidden)),
            cache_spec, cache_spec,
        ],
        out_specs=[whole((n_tok, hidden)), whole((n_tok, hidden)), whole((2, ep_size, n_tok)), cache_spec, cache_spec],
        out_shape=[
            jax.ShapeDtypeStruct((n_tok, hidden), BF16), jax.ShapeDtypeStruct((n_tok, hidden), BF16), jax.ShapeDtypeStruct((2, ep_size, n_tok), F32),
            jax.ShapeDtypeStruct(kt.shape, BF16), jax.ShapeDtypeStruct(vt.shape, BF16),
        ],
        scratch_shapes=[
            pltpu.VMEM((n_tok, hidden), BF16), pltpu.VMEM((head_dim // 2, n_tok), F32), pltpu.VMEM((head_dim // 2, n_tok), F32),
            pltpu.VMEM((head_dim, 128), F32), pltpu.VMEM((head_dim, 128), F32), pltpu.VMEM((head_dim, n_tok), BF16),
            pltpu.VMEM((2, head_dim, n_tok), F32), pltpu.VMEM((2, head_dim, n_tok), BF16), pltpu.VMEM((2, head_dim, n_tok), BF16),
            pltpu.VMEM((2, n_slots, n_tok), F32), pltpu.VMEM((n_tok, w_q.shape[1]), BF16), pltpu.VMEM(w_o.shape, BF16), pltpu.SemaphoreType.DMA,
        ],
        name="attend",
    )(freq, x_in, cache_len.reshape(1, n_tok), topk_idx.T, ln_attn.reshape(1, hidden), q_norm.reshape(1, head_dim), k_norm.reshape(1, head_dim),
      w_q, w_k, w_v, w_o, ln_moe.reshape(1, hidden), w_router.T, kt, vt)
    x1, h2, ri, kto, vto = out
    return x1, h2, ri, kto.transpose(3, 0, 1, 2), vto.transpose(3, 0, 1, 2)


def moe_kernel(n_chip, h2_ref, ri_ref, x1_ref, wg_hbm, wu_hbm, wd_hbm, out_ref,
               wg, wu, wd, hbuf, gbuf, xm, gm, m_scr, ybuf, y_near, y_far, y_peer, y_own, s_out, s_in,
               w_sem, send_h, recv_h, send_p, recv_p, send_g, recv_g, send_n, recv_n, send_f, recv_f, send_y, recv_y, send_s, recv_s):
    ep = lax.axis_index("ep")
    core = lax.rem(ep, 2)
    chip = ep // 2
    right = lax.rem(chip + 1, n_chip)
    left = lax.rem(chip + n_chip - 1, n_chip)
    opp = lax.rem(chip + 2, n_chip)
    other = 1 - core
    n_tok, hidden = h2_ref.shape
    hb = n_tok // 2
    e_local = wg.shape[0] // hidden
    ff = wg.shape[1]

    def dev(ch, co):
        return {"ep": ch * 2 + co}

    def rcopy(src, dst, ssem, rsem, ch, co):
        return pltpu.make_async_remote_copy(src_ref=src, dst_ref=dst, send_sem=ssem, recv_sem=rsem, device_id=dev(ch, co), device_id_type=MESH)

    top = pl.ds(0, hb)
    bot = pl.ds(hb, hb)

    w_copies = [pltpu.make_async_copy(wg_hbm, wg, w_sem.at[0]), pltpu.make_async_copy(wu_hbm, wu, w_sem.at[1]), pltpu.make_async_copy(wd_hbm, wd, w_sem.at[2])]

    dispatch = {
        1: rcopy(h2_ref.at[top], hbuf.at[1, top], send_h.at[1], recv_h.at[1], right, core),
        2: rcopy(h2_ref.at[bot], hbuf.at[2, top], send_h.at[2], recv_h.at[2], left, core),
        5: rcopy(h2_ref.at[bot], hbuf.at[5, top], send_h.at[5], recv_h.at[5], right, core),
        6: rcopy(h2_ref.at[top], hbuf.at[6, top], send_h.at[6], recv_h.at[6], left, core),
        3: rcopy(hbuf.at[1, top], hbuf.at[3, top], send_h.at[3], recv_h.at[3], right, core),
        4: rcopy(hbuf.at[2, top], hbuf.at[4, top], send_h.at[4], recv_h.at[4], left, core),
    }
    to_peer = {u: rcopy(hbuf.at[u, top], hbuf.at[u, bot], send_p.at[u], recv_p.at[u], chip, other) for u in range(1, 7)}
    to_peer[7] = rcopy(h2_ref, hbuf.at[7], send_p.at[7], recv_p.at[7], chip, other)
    gate = []
    for u, hf, ch in ((1, 0, right), (2, 1, left), (3, 0, opp), (4, 1, opp), (5, 1, right), (6, 0, left)):
        for q, co in ((0, core), (1, other)):
            gate.append(rcopy(ri_ref.at[:, :, pl.ds(hf * hb, hb)], gbuf.at[u, :, :, pl.ds(q * hb, hb)], send_g.at[2 * u + q], recv_g.at[2 * u + q], ch, co))
    gate.append(rcopy(ri_ref, gbuf.at[7], send_g.at[14], recv_g.at[14], chip, other))

    near = {}
    far = {}
    for u, ch, slot in ((1, left, 0), (2, right, 1)):
        near[u] = [rcopy(ybuf.at[u, top], y_near.at[slot, core], send_n.at[slot, 0], recv_n.at[slot, core], ch, core),
                   rcopy(ybuf.at[u, bot], y_near.at[slot, core], send_n.at[slot, 1], recv_n.at[slot, core], ch, other)]
    for u, ch, slot in ((3, right, 1), (4, left, 0)):
        far[u] = [rcopy(ybuf.at[u, top], y_far.at[slot, core], send_f.at[slot, 0], recv_f.at[slot, core], ch, core),
                  rcopy(ybuf.at[u, bot], y_far.at[slot, core], send_f.at[slot, 1], recv_f.at[slot, core], ch, other)]
    peer_y = {5: rcopy(ybuf.at[5, bot], y_peer.at[0], send_y.at[0], recv_y.at[0], chip, other),
              6: rcopy(ybuf.at[6, bot], y_peer.at[1], send_y.at[1], recv_y.at[1], chip, other),
              7: rcopy(ybuf.at[7], y_own, send_y.at[2], recv_y.at[2], chip, other)}
    sums = {0: rcopy(s_out.at[0], s_in.at[1], send_s.at[0], recv_s.at[1], left, core),
            1: rcopy(s_out.at[1], s_in.at[0], send_s.at[1], recv_s.at[0], right, core)}

    for c in w_copies:
        c.start()
    barrier = pltpu.get_barrier_semaphore()
    for d in range(1, 2 * n_chip):
        pl.semaphore_signal(barrier, inc=1, device_id={"ep": lax.rem(ep + d, 2 * n_chip)}, device_id_type=MESH)
    pl.semaphore_wait(barrier, 2 * n_chip - 1)

    dispatch[1].start()
    dispatch[2].start()
    for c in gate:
        c.start()
    dispatch[5].start()
    dispatch[6].start()
    to_peer[7].start()
    hbuf[0] = h2_ref[...]
    gbuf[0] = ri_ref[...]

    dev_iota = lax.broadcasted_iota(jnp.int32, (2 * n_chip, 128), 0)

    def row_of(block, d):
        return jnp.sum(jnp.where(dev_iota == d, block, 0.0), axis=0, keepdims=True)

    def columns(rows):
        rows = rows + [jnp.zeros((128 - len(rows), 128), F32)]
        return jnp.concatenate(rows, axis=0).T

    def compute(u):
        for hf in range(2):
            rs = pl.ds(hf * hb, hb)
            ids = row_of(gbuf[u, 1, :, pl.ds(hf * hb, hb)], ep)
            cols = columns([(ids == float(e)).astype(F32) for e in range(e_local)])
            for e in range(e_local):
                keep = jnp.broadcast_to(cols[:, e:e + 1], (hb, 128)).astype(BF16)
                m_scr[e, rs, :] = keep
                for b in range(hidden // 128):
                    xm[rs, e * hidden + b * 128:e * hidden + (b + 1) * 128] = hbuf[u, rs, b * 128:(b + 1) * 128] * keep

        def up_tile(n, carry):
            cs = pl.ds(pl.multiple_of(n * 256, 256), 256)
            a = jnp.dot(xm[...], wg[:, cs], preferred_element_type=F32)
            b = jnp.dot(xm[...], wu[:, cs], preferred_element_type=F32)
            g = (a * (1.0 / (1.0 + jnp.exp(-a))) * b).astype(BF16)
            for e in range(e_local):
                for q in range(2):
                    gm[:, pl.ds(pl.multiple_of(n * 256, 256) + e * ff + q * 128, 128)] = g[:, q * 128:(q + 1) * 128] * m_scr[e]
            return carry

        lax.fori_loop(0, ff // 256, up_tile, 0)

        def down_tile(n, carry):
            cs = pl.ds(pl.multiple_of(n * 256, 256), 256)
            ybuf[u, :, cs] = jnp.dot(gm[...], wd[:, cs], preferred_element_type=F32).astype(BF16)
            return carry

        lax.fori_loop(0, hidden // 256, down_tile, 0)

    def gate_cols(u, lanes, devs):
        blk = gbuf[u, 0, :, lanes]
        return columns([row_of(blk, d) for d in devs])

    def wait_gate(u):
        if u == 7:
            gate[12].wait_recv()
        else:
            gate[2 * (u - 1)].wait_recv()
            gate[2 * (u - 1) + 1].wait_recv()

    def before(u):
        if u == 0:
            for c in w_copies:
                c.wait()
        if u == 1:
            for v in (1, 2):
                dispatch[v].wait_recv()
                dispatch[v + 2].start()
                to_peer[v].start()
        if u == 2:
            for v in (5, 6):
                dispatch[v].wait_recv()
                to_peer[v].start()
        if u == 3:
            for v in (3, 4):
                dispatch[v].wait_recv()
                to_peer[v].start()
        if u >= 1:
            to_peer[u].wait_recv()
            wait_gate(u)

    def after(u):
        if u in (1, 2):
            for c in near[u]:
                c.start()
        if u in (3, 4):
            for c in far[u]:
                c.start()
        if u in (5, 6, 7):
            peer_y[u].start()

    def unit(u, carry):
        for v in range(8):
            pl.when(u == v)(functools.partial(before, v))
        compute(u)
        for v in range(1, 8):
            pl.when(u == v)(functools.partial(after, v))
        return carry

    lax.fori_loop(0, 8, unit, 0)

    for slot, u, ch in ((0, 5, right), (1, 6, left)):
        peer_y[u].wait_recv()
        for co in range(2):
            rcopy(y_far.at[slot, co], y_far.at[slot, co], send_f.at[slot, co], recv_f.at[slot, co], ch, core).wait_recv()
        cols = gate_cols(u, pl.ds(0, 128), [ep, chip * 2 + other, ch * 2, ch * 2 + 1])
        s_out[slot] = (ybuf[u, top, :].astype(F32) * cols[:, 0:1] + y_peer[slot].astype(F32) * cols[:, 1:2]
                       + y_far[slot, 0].astype(F32) * cols[:, 2:3] + y_far[slot, 1].astype(F32) * cols[:, 3:4])
        sums[slot].start()

    peer_y[7].wait_recv()
    for hf, ch in ((0, right), (1, left)):
        rs = pl.ds(hf * hb, hb)
        for co in range(2):
            rcopy(y_near.at[hf, co], y_near.at[hf, co], send_n.at[hf, co], recv_n.at[hf, co], ch, core).wait_recv()
        cols = gate_cols(0, rs, [ep, chip * 2 + other, ch * 2, ch * 2 + 1])
        acc = (ybuf[0, rs, :].astype(F32) * cols[:, 0:1] + y_own[rs, :].astype(F32) * cols[:, 1:2]
               + y_near[hf, 0].astype(F32) * cols[:, 2:3] + y_near[hf, 1].astype(F32) * cols[:, 3:4])
        total = x1_ref[rs, :].astype(F32) + acc
        sums[1 - hf].wait_recv()
        out_ref[rs, :] = (total + s_in[hf]).astype(BF16)

    for group in (list(dispatch.values()), gate, list(to_peer.values()), near[1], near[2], far[3], far[4], list(peer_y.values()), list(sums.values())):
        for c in group:
            c.wait_send()


def moe(h2, ri, x1, w_gate, w_up, w_down, ep_size):
    n_tok, hidden = h2.shape
    e_local, _, ff = w_gate.shape
    hb = n_tok // 2
    dma = pltpu.SemaphoreType.DMA
    vmem = pl.BlockSpec(memory_space=pltpu.VMEM)
    hbm = pl.BlockSpec(memory_space=pl.ANY)
    return pl.pallas_call(
        functools.partial(moe_kernel, ep_size // 2),
        out_shape=jax.ShapeDtypeStruct((n_tok, hidden), BF16),
        in_specs=[vmem, vmem, vmem, hbm, hbm, hbm],
        out_specs=vmem,
        scratch_shapes=[
            pltpu.VMEM((e_local * hidden, ff), BF16), pltpu.VMEM((e_local * hidden, ff), BF16), pltpu.VMEM((e_local * ff, hidden), BF16),
            pltpu.VMEM((8, n_tok, hidden), BF16), pltpu.VMEM((8, 2, ep_size, n_tok), F32),
            pltpu.VMEM((n_tok, e_local * hidden), BF16), pltpu.VMEM((n_tok, e_local * ff), BF16), pltpu.VMEM((e_local, n_tok, 128), BF16),
            pltpu.VMEM((8, n_tok, hidden), BF16), pltpu.VMEM((2, 2, hb, hidden), BF16), pltpu.VMEM((2, 2, hb, hidden), BF16), pltpu.VMEM((2, hb, hidden), BF16), pltpu.VMEM((n_tok, hidden), BF16),
            pltpu.VMEM((2, hb, hidden), F32), pltpu.VMEM((2, hb, hidden), F32),
            dma((3,)), dma((8,)), dma((8,)), dma((8,)), dma((8,)), dma((15,)), dma((15,)), dma((2, 2)), dma((2, 2)), dma((2, 2)), dma((2, 2)), dma((3,)), dma((3,)), dma((2,)), dma((2,)),
        ],
        compiler_params=pltpu.CompilerParams(collective_id=0, has_side_effects=True),
        name="moe",
    )(h2, ri, x1, w_gate.reshape(e_local * hidden, ff), w_up.reshape(e_local * hidden, ff), w_down.reshape(e_local * ff, hidden))


def solution(mesh):
    ep_size = mesh.shape['ep']
    row_spec = P(('dp', 'ep'))
    replicated = P()
    expert_spec = P('ep')
    in_specs = (row_spec,) * 5 + (replicated,) * 9 + (expert_spec,) * 3

    def device_step(x_in, k_cache, v_cache, cache_len, topk_idx, ln_attn, w_q, w_k, w_v, q_norm, k_norm, w_o, ln_moe, w_router, w_gate, w_up, w_down):
        x1, h2, ri, k_new, v_new = attention(x_in, k_cache, v_cache, cache_len, topk_idx, ln_attn, w_q, w_k, w_v, q_norm, k_norm, w_o, ln_moe, w_router, ep_size)
        return moe(h2, ri, x1, w_gate, w_up, w_down, ep_size), k_new, v_new

    return jax.shard_map(device_step, mesh=mesh, in_specs=in_specs, out_specs=(row_spec,) * 3, check_vma=False)
```

time: 366 us -> 101 us (0.28)
  local copies, waits for them, and re-layouts: 146 us -> 4.42 us
  waiting for transfers between devices: 67.1 us -> 0 us
  other arithmetic: 57.1 us -> 0 us
  Pallas kernels: 42.3 us -> 95.3 us
  matrix products: 32.9 us -> 0 us
  starting transfers between devices: 16.2 us -> 0 us
    pallas_call x0 -> x2, Pallas kernels: none -> 95.3 us  [the longest x1 70.4 us: moe(): pl.pallas_call(functools.partial(moe_kernel, ep_size // 2), out_shape=jax...]
    gather x12 -> x0, local copies, waits for them, and re-layouts: 91.9 us -> none  [the longest x5 17.2 us: route_gate(): jnp.take_along_axis(logits, topk_idx, axis=1)]
    all_to_all x3 -> x0, waiting for transfers between devices: 67.1 us -> none  [the longest x1 36.4 us: device_step(): lax.all_to_all(send_rows, 'ep', 0, 0, tiled=True)]
    select_n x2 -> x0, local copies, waits for them, and re-layouts: 48.1 us -> none  [the longest x1 24.1 us: attend_block(): k_full = jnp.where(is_new, k_new[:, None], k_cache)]
    another operation x3 -> x0, Pallas kernels: 40.9 us -> none
    dot_general x6 -> x0, matrix products: 17.5 us -> none  [the longest x1 10 us: attend_block(): jnp.einsum('bgrs,bsgd->bgrd', attn_prob, v_full, preferred_element_type=j...]
    select_n x6 -> x0, other arithmetic: 16.2 us -> none  [the longest x1 11.7 us: attend_block(): k_full = jnp.where(is_new, k_new[:, None], k_cache)]
    all_to_all x3 -> x0, starting transfers between devices: 16.2 us -> none  [the longest x1 6.01 us: device_step(): lax.all_to_all(send_ids, 'ep', 0, 0, tiled=True).reshape(ep_size * cap_rows)]
  transfers between devices with their start and end apart: 3 -> 0, of which waited for: 2 -> 0; matrix products, arithmetic and copies ran while one was open for 39% -> 0% of each run, Pallas kernels for 0% -> 0%
where the time goes in v1:
time: 101 us; the launch traced here: 100 us
  Pallas kernels  95.3 us (94%)
  local copies, waits for them, and re-layouts  4.42 us (4%)
    pallas_call x1, Pallas kernels, moe(): pl.pallas_call(functools.partial(moe_kernel, ep_size // 2), out_shape=jax...  70.4 us
    pallas_call x1, Pallas kernels, attention(): pl.pallas_call(attn_kernel, grid=(kv_heads,), in_specs=[whole(freq.shape)...  24.9 us

profile of v1, /device:TPU:81, one launch (start us, length us, event | category | flops | bytes accessed | tf_op | source)
XLA Modules:
  0.0 100.4 jit_solution(9381121754879169090)
XLA Ops:
  0.6 1.3 %reshape.31.lna_ref = bf16[1,1024]{1,0:T(2,128)(2,1)} reshape(bf16[1024]{0:T(1024)(128)(2,1)} %param.23) | data formatting | bytes 4096 | tf_op jit(solution)/shard_map/reshape | solution.py:172
  1.9 1.3 %reshape.34.lnm_ref = bf16[1,1024]{1,0:T(2,128)(2,1)} reshape(bf16[1024]{0:T(1024)(128)(2,1)} %param.30) | data formatting | bytes 4096 | tf_op jit(solution)/shard_map/reshape | solution.py:173
  3.2 24.9 %attend.1 = (bf16[256,1024]{1,0:T(8,128)(2,1)}, bf16[256,1024]{1,0:T(8,128)(2,1)}, f32[2,8,256]{2,1,0:T(8,128)}, bf16[32,8,64,256]{3,2,1,0:T(8,128)(2,1)}, bf16[32,8,64,256]{3,2,1,0:T(8,128)(2,1)}) custom-call(f32[32,128]{1,0:T(8,128)} %constant.2.clone.freq_ref, bf16[256,1024]{1,0:T(8,128)(2,1)} %x_ref.1, s32[1,256]{1,0:T(1,128)} %bitcast.19, ...), custom_call_target="tpu_custom_call" | custom-call | tf_op jit(solution)/shard_map/attend/pallas_call | solution.py:152
  28.0 70.4 %moe.1 = bf16[256,1024]{1,0:T(8,128)(2,1)} custom-call(bf16[256,1024]{1,0:T(8,128)(2,1)} %get-tuple-element.8.h2_ref, f32[2,8,256]{2,1,0:T(8,128)} %get-tuple-element.9.ri_ref, bf16[256,1024]{1,0:T(8,128)(2,1)} %get-tuple-element.10.x1_ref, bf16[4096,512]{1,0:T(8,128)(2,1)} %bitcast.14, bf16[4096,512]{1,0:T(8,128)(2,1)} %bitcast.15, bf16[2048,1024]{1,0:T(8,128)(2,1)} %bitcast.16), custom_call_target="tpu_custom_call" | custom-call | tf_op jit(solution)/shard_map/moe/pallas_call | solution.py:375
  98.5 1.9 %copy.22 = bf16[256,1024]{1,0:T(8,128)(2,1)} copy(bf16[256,1024]{1,0:T(8,128)(2,1)} %moe.1) | data formatting | bytes 1048576

commit v2 on v1

v2 whole, which is shorter than its diff:
```python
import functools

import jax
import jax.numpy as jnp
import numpy as np
from jax import lax
from jax.experimental import pallas as pl
from jax.experimental.pallas import tpu as pltpu
from jax.sharding import PartitionSpec as P

ROPE_BASE = 1000000.0
NORM_EPS = 1e-6
F32 = jnp.float32
BF16 = jnp.bfloat16
MESH = pl.DeviceIdType.MESH


def sublane_sums(parts):
    row = lax.broadcasted_iota(jnp.int32, parts[0].shape, 0)
    for d in (1, 2, 4):
        low = (row & d) == 0
        parts = [jnp.where(low, a, b) + pltpu.roll(jnp.where(low, b, a), d, 0) for a, b in zip(parts[0::2], parts[1::2])]
    return parts[0]


def attn_kernel(freq_ref, x_ref, len_ref, topk_ref, lna_ref, qn_ref, kn_ref, lnm_ref, wr_ref, wq_hbm, wk_hbm, wv_hbm, wo_hbm, kc_hbm, vc_hbm,
                x1_ref, h2_ref, ri_ref, kco_hbm, vco_hbm,
                wq_scr, wk_scr, wv_scr, wo_scr, kbuf, vbuf, h_scr, cos_scr, sin_scr, qg_scr, kg_scr, len_scr, q_scr, kn_scr, vn_scr, s_scr, o_scr,
                w_sem, kin_sem, vin_sem, kout_sem, vout_sem):
    n_tok = x_ref.shape[0]
    n_head, n_slots, head_dim, _ = kbuf.shape
    half = head_dim // 2
    n_lt = n_tok // 128
    early = 1
    ahead = 4

    w_copies = [pltpu.make_async_copy(src, dst, w_sem.at[i]) for i, (src, dst) in enumerate(((wk_hbm, wk_scr), (wv_hbm, wv_scr), (wq_hbm, wq_scr), (wo_hbm, wo_scr)))]

    def reads(g):
        return (pltpu.make_async_copy(kc_hbm.at[:, g], kbuf.at[g], kin_sem.at[g]), pltpu.make_async_copy(vc_hbm.at[:, g], vbuf.at[g], vin_sem.at[g]))

    def writes(g):
        return (pltpu.make_async_copy(kbuf.at[g], kco_hbm.at[:, g], kout_sem.at[g]), pltpu.make_async_copy(vbuf.at[g], vco_hbm.at[:, g], vout_sem.at[g]))

    for c in w_copies[:3]:
        c.start()
    for g in range(early):
        for c in reads(g):
            c.start()

    xf = x_ref[...].astype(F32)
    ms = jnp.mean(xf * xf, axis=1, keepdims=True)
    h_scr[...] = (xf * lax.rsqrt(ms + NORM_EPS) * lna_ref[...].astype(F32)[None, :]).astype(BF16)
    lens = len_ref[...].astype(F32)
    angles = jnp.concatenate([freq_ref[...]] * n_lt, axis=1) * lens
    cos_scr[...] = jnp.cos(angles)
    sin_scr[...] = jnp.sin(angles)
    for src, dst in ((qn_ref, qg_scr), (kn_ref, kg_scr)):
        row = src[...].astype(F32)
        dst[...] = jnp.broadcast_to(jnp.concatenate([row, row], axis=1), (128, 128)).T[:head_dim]
    len_scr[...] = jnp.broadcast_to(lens, (16, n_tok)).astype(BF16)

    def head_rope(block, gain_scr):
        ms = jnp.mean(block * block, axis=0, keepdims=True)
        gain = jnp.concatenate([gain_scr[...]] * n_lt, axis=1)
        block = block * lax.rsqrt(ms + NORM_EPS) * gain
        lo, hi = block[:half], block[half:]
        cosv, sinv = cos_scr[...], sin_scr[...]
        return jnp.concatenate([lo * cosv - hi * sinv, hi * cosv + lo * sinv], axis=0).astype(BF16)

    per = 256 // head_dim
    for c in w_copies[:3]:
        c.wait()
    for g in range(early, ahead):
        for c in reads(g):
            c.start()
    w_copies[3].start()

    def project(w_scr, i):
        cols = pl.ds(pl.multiple_of(i * 256, 256), 256)
        return jnp.dot(h_scr[...], w_scr[:, cols], preferred_element_type=F32).T

    def kv_proj(i, carry):
        k_t = project(wk_scr, i)
        v_t = project(wv_scr, i)
        for j in range(per):
            kn_scr[i * per + j] = head_rope(k_t[j * head_dim:(j + 1) * head_dim], kg_scr)
            vn_scr[i * per + j] = v_t[j * head_dim:(j + 1) * head_dim].astype(BF16)
        return carry

    def q_proj(i, carry):
        q_t = project(wq_scr, i)
        for j in range(per):
            q_scr[i * per + j] = head_rope(q_t[j * head_dim:(j + 1) * head_dim], qg_scr).astype(F32)
        return carry

    lax.fori_loop(0, n_head // per, kv_proj, 0, unroll=True)
    lax.fori_loop(0, 2 * n_head // per, q_proj, 0, unroll=True)

    tiles = [pl.ds(r * 16, 16) for r in range(head_dim // 16)]

    def head(g, carry):
        @pl.when(g + ahead < n_head)
        def _():
            for c in reads(g + ahead):
                c.start()

        for c in reads(g):
            c.wait()

        for lt in range(n_lt):
            lanes = pl.ds(lt * 128, 128)

            def score_block(i, carry):
                parts = [[], []]
                for si in range(8):
                    s = i * 8 + si
                    hit = len_scr[:, lanes] == s.astype(F32).astype(BF16)
                    accs = [None, None]
                    for t in tiles:
                        kb = kbuf[g, s, t, lanes]
                        kbuf[g, s, t, lanes] = jnp.where(hit, kn_scr[g, t, lanes], kb)
                        kf = kb.astype(F32)
                        for j in range(2):
                            prod = kf * q_scr[2 * g + j, t, lanes]
                            accs[j] = prod if accs[j] is None else accs[j] + prod
                    for j in range(2):
                        parts[j].append(accs[j][:8] + accs[j][8:])
                for j in range(2):
                    s_scr[j, pl.ds(pl.multiple_of(i * 8, 8), 8), lanes] = sublane_sums(parts[j])
                return carry

            lax.fori_loop(0, n_slots // 8, score_block, 0)
            slot = lax.broadcasted_iota(jnp.int32, (n_slots, 128), 0)
            len_row = len_ref[:, lanes]
            kn = kn_scr[g, :, lanes].astype(F32)
            vn = vn_scr[g, :, lanes].astype(F32)
            accs = []
            for j in range(2):
                fresh = jnp.sum(kn * q_scr[2 * g + j, :, lanes], axis=0, keepdims=True)
                sc = jnp.where(slot == len_row, fresh, s_scr[j, :, lanes]) * (head_dim ** -0.5)
                sc = jnp.where(slot <= len_row, sc, -1e30)
                ex = jnp.exp(sc - jnp.max(sc, axis=0, keepdims=True))
                pr = (ex / jnp.sum(ex, axis=0, keepdims=True)).astype(BF16).astype(F32)
                accs.append(jnp.sum(jnp.where(slot == len_row, pr, 0.0), axis=0, keepdims=True) * vn)
                s_scr[j, :, lanes] = jnp.where(slot == len_row, 0.0, pr)

            def value_block(i, accs):
                accs = [[a[r * 16:(r + 1) * 16] for r in range(len(tiles))] for a in accs]
                prob = [s_scr[j, pl.ds(pl.multiple_of(i * 8, 8), 8), lanes] for j in range(2)]
                for si in range(8):
                    s = i * 8 + si
                    hit = len_scr[:, lanes] == s.astype(F32).astype(BF16)
                    for r, t in enumerate(tiles):
                        vb = vbuf[g, s, t, lanes]
                        vbuf[g, s, t, lanes] = jnp.where(hit, vn_scr[g, t, lanes], vb)
                        vf = vb.astype(F32)
                        for j in range(2):
                            accs[j][r] = accs[j][r] + prob[j][si:si + 1] * vf
                return tuple(jnp.concatenate(a, axis=0) for a in accs)

            accs = lax.fori_loop(0, n_slots // 8, value_block, tuple(accs))
            o_scr[pl.ds(lt * 128, 128), pl.ds(pl.multiple_of(g * 128, 128), 128)] = jnp.concatenate(accs, axis=0).T.astype(BF16)
        for c in writes(g):
            c.start()
        return carry

    lax.fori_loop(0, n_head, head, 0)

    w_copies[3].wait()
    x1 = (x_ref[...].astype(F32) + jnp.dot(o_scr[...], wo_scr[...], preferred_element_type=F32)).astype(BF16)
    x1_ref[...] = x1
    xf = x1.astype(F32)
    ms = jnp.mean(xf * xf, axis=1, keepdims=True)
    h2 = (xf * lax.rsqrt(ms + NORM_EPS) * lnm_ref[...].astype(F32)[None, :]).astype(BF16)
    h2_ref[...] = h2
    logits = lax.dot_general(wr_ref[...], h2, (((1,), (1,)), ((), ())), preferred_element_type=F32)
    top_k = topk_ref.shape[0]
    n_exp = wr_ref.shape[0]
    n_dev = ri_ref.shape[1]
    e_local = n_exp // n_dev
    exp_id = lax.broadcasted_iota(jnp.int32, (n_exp, n_tok), 0)
    picked = [jnp.sum(jnp.where(exp_id == topk_ref[pl.ds(k, 1), :], logits, 0.0), axis=0, keepdims=True) for k in range(top_k)]
    picked = jnp.concatenate(picked, axis=0)
    ex = jnp.exp(picked - jnp.max(picked, axis=0, keepdims=True))
    gate = ex / jnp.sum(ex, axis=0, keepdims=True)
    dev_id = lax.broadcasted_iota(jnp.int32, (n_dev, n_tok), 0)
    r_dev = jnp.zeros((n_dev, n_tok), F32)
    i_dev = jnp.zeros((n_dev, n_tok), F32)
    for k in range(top_k):
        idx = topk_ref[pl.ds(k, 1), :]
        dev = idx // e_local
        mine = dev_id == dev
        r_dev = r_dev + jnp.where(mine, gate[k:k + 1], 0.0)
        i_dev = i_dev + jnp.where(mine, (idx - dev * e_local).astype(F32), 0.0)
    ri_ref[0] = r_dev
    ri_ref[1] = i_dev

    def drain(g, carry):
        for c in writes(g):
            c.wait()
        return carry

    lax.fori_loop(0, n_head, drain, 0)


def attention(x_in, k_cache, v_cache, cache_len, topk_idx, ln_attn, w_q, w_k, w_v, q_norm, k_norm, w_o, ln_moe, w_router, ep_size):
    n_tok, hidden = x_in.shape
    _, n_slots, kv_heads, head_dim = k_cache.shape
    freq = np.float32(ROPE_BASE) ** (-np.arange(head_dim // 2, dtype=np.float32) * np.float32(2.0) / np.float32(head_dim))
    freq = jnp.asarray(np.ascontiguousarray(np.broadcast_to(freq[:, None], (head_dim // 2, 128))), F32)
    kt = k_cache.transpose(1, 2, 3, 0)
    vt = v_cache.transpose(1, 2, 3, 0)
    vmem = pl.BlockSpec(memory_space=pltpu.VMEM)
    hbm = pl.BlockSpec(memory_space=pl.ANY)
    dma = pltpu.SemaphoreType.DMA
    out = pl.pallas_call(
        attn_kernel,
        in_specs=[vmem] * 9 + [hbm] * 6,
        out_specs=[vmem, vmem, vmem, hbm, hbm],
        out_shape=[
            jax.ShapeDtypeStruct((n_tok, hidden), BF16), jax.ShapeDtypeStruct((n_tok, hidden), BF16), jax.ShapeDtypeStruct((2, ep_size, n_tok), F32),
            jax.ShapeDtypeStruct(kt.shape, BF16), jax.ShapeDtypeStruct(vt.shape, BF16),
        ],
        scratch_shapes=[
            pltpu.VMEM(w_q.shape, BF16), pltpu.VMEM(w_k.shape, BF16), pltpu.VMEM(w_v.shape, BF16), pltpu.VMEM(w_o.shape, BF16),
            pltpu.VMEM((kv_heads, n_slots, head_dim, n_tok), BF16), pltpu.VMEM((kv_heads, n_slots, head_dim, n_tok), BF16),
            pltpu.VMEM((n_tok, hidden), BF16), pltpu.VMEM((head_dim // 2, n_tok), F32), pltpu.VMEM((head_dim // 2, n_tok), F32),
            pltpu.VMEM((head_dim, 128), F32), pltpu.VMEM((head_dim, 128), F32), pltpu.VMEM((16, n_tok), BF16),
            pltpu.VMEM((2 * kv_heads, head_dim, n_tok), F32), pltpu.VMEM((kv_heads, head_dim, n_tok), BF16), pltpu.VMEM((kv_heads, head_dim, n_tok), BF16),
            pltpu.VMEM((2, n_slots, n_tok), F32), pltpu.VMEM((n_tok, w_q.shape[1]), BF16),
            dma((4,)), dma((kv_heads,)), dma((kv_heads,)), dma((kv_heads,)), dma((kv_heads,)),
        ],
        name="attend",
    )(freq, x_in, cache_len.reshape(1, n_tok), topk_idx.T, ln_attn, q_norm.reshape(1, head_dim), k_norm.reshape(1, head_dim),
      ln_moe, w_router.T, w_q, w_k, w_v, w_o, kt, vt)
    x1, h2, ri, kto, vto = out
    return x1, h2, ri, kto.transpose(3, 0, 1, 2), vto.transpose(3, 0, 1, 2)


def moe_kernel(n_chip, h2_ref, ri_ref, x1_ref, wg_hbm, wu_hbm, wd_hbm, out_ref,
               wg, wu, wd, hbuf, gsrc, gbuf, xm, gm, m_scr, ybuf, y_near, y_far, y_peer, y_own, s_out, s_in, acc_scr,
               w_sem, send_h, recv_h, send_p, recv_p, send_g, recv_g, send_n, recv_n, send_f, recv_f, send_y, recv_y, send_s, recv_s):
    ep = lax.axis_index("ep")
    core = lax.rem(ep, 2)
    chip = ep // 2
    right = lax.rem(chip + 1, n_chip)
    left = lax.rem(chip + n_chip - 1, n_chip)
    opp = lax.rem(chip + 2, n_chip)
    other = 1 - core
    n_tok, hidden = h2_ref.shape
    hb = n_tok // 2
    qb = hb // 2
    e_local = wg.shape[0] // hidden
    ff = wg.shape[1]

    def dev(ch, co):
        return {"ep": ch * 2 + co}

    def rcopy(src, dst, ssem, rsem, ch, co):
        return pltpu.make_async_remote_copy(src_ref=src, dst_ref=dst, send_sem=ssem, recv_sem=rsem, device_id=dev(ch, co), device_id_type=MESH)

    top = pl.ds(0, hb)
    bot = pl.ds(hb, hb)

    w_copies = [pltpu.make_async_copy(wg_hbm, wg, w_sem.at[0]), pltpu.make_async_copy(wu_hbm, wu, w_sem.at[1]), pltpu.make_async_copy(wd_hbm, wd, w_sem.at[2])]

    dispatch = {
        1: rcopy(h2_ref.at[top], hbuf.at[1, top], send_h.at[1], recv_h.at[1], right, core),
        2: rcopy(h2_ref.at[bot], hbuf.at[2, top], send_h.at[2], recv_h.at[2], left, core),
        5: rcopy(h2_ref.at[bot], hbuf.at[5, top], send_h.at[5], recv_h.at[5], right, core),
        6: rcopy(h2_ref.at[top], hbuf.at[6, top], send_h.at[6], recv_h.at[6], left, core),
        3: rcopy(hbuf.at[1, top], hbuf.at[3, top], send_h.at[3], recv_h.at[3], right, core),
        4: rcopy(hbuf.at[2, top], hbuf.at[4, top], send_h.at[4], recv_h.at[4], left, core),
    }
    to_peer = {u: rcopy(hbuf.at[u, top], hbuf.at[u, bot], send_p.at[u], recv_p.at[u], chip, other) for u in range(1, 7)}
    to_peer[7] = rcopy(h2_ref, hbuf.at[7], send_p.at[7], recv_p.at[7], chip, other)
    gate = {}
    for rel, ch in ((0, chip), (1, right), (2, opp), (3, left)):
        for q, co in ((0, core), (1, other)):
            if rel or q:
                gate[2 * rel + q] = rcopy(ri_ref, gsrc.at[2 * rel + q], send_g.at[2 * rel + q], recv_g.at[2 * rel + q], ch, co)

    near = {}
    far = {}
    for u, ch, slot in ((1, left, 0), (2, right, 1)):
        near[u] = [rcopy(ybuf.at[u, top], y_near.at[slot, core], send_n.at[slot, 0], recv_n.at[slot, core], ch, core),
                   rcopy(ybuf.at[u, bot], y_near.at[slot, core], send_n.at[slot, 1], recv_n.at[slot, core], ch, other)]
    for u, ch, slot in ((3, right, 1), (4, left, 0)):
        far[u] = []
        for p in range(2):
            rows = pl.ds(p * qb, qb)
            far[u].append(rcopy(ybuf.at[u, rows], y_far.at[slot, core, rows], send_f.at[slot, p, 0], recv_f.at[slot, core, p], ch, core))
            far[u].append(rcopy(ybuf.at[u, pl.ds(hb + p * qb, qb)], y_far.at[slot, core, rows], send_f.at[slot, p, 1], recv_f.at[slot, core, p], ch, other))
    peer_y = {5: rcopy(ybuf.at[5, bot], y_peer.at[0], send_y.at[0], recv_y.at[0], chip, other),
              6: rcopy(ybuf.at[6, bot], y_peer.at[1], send_y.at[1], recv_y.at[1], chip, other),
              7: rcopy(ybuf.at[7], y_own, send_y.at[2], recv_y.at[2], chip, other)}
    sums = {}
    for p in range(2):
        rows = pl.ds(p * qb, qb)
        sums[0, p] = rcopy(s_out.at[0, rows], s_in.at[1, rows], send_s.at[0, p], recv_s.at[1, p], left, core)
        sums[1, p] = rcopy(s_out.at[1, rows], s_in.at[0, rows], send_s.at[1, p], recv_s.at[0, p], right, core)

    for c in w_copies:
        c.start()
    barrier = pltpu.get_barrier_semaphore()
    for d in range(1, 2 * n_chip):
        pl.semaphore_signal(barrier, inc=1, device_id={"ep": lax.rem(ep + d, 2 * n_chip)}, device_id_type=MESH)
    pl.semaphore_wait(barrier, 2 * n_chip - 1)

    dispatch[1].start()
    dispatch[2].start()
    for c in gate.values():
        c.start()
    dispatch[5].start()
    dispatch[6].start()
    to_peer[7].start()
    hbuf[0] = h2_ref[...]
    gbuf[0] = ri_ref[...]

    dev_iota = lax.broadcasted_iota(jnp.int32, (2 * n_chip, 128), 0)

    def row_of(block, d):
        return jnp.sum(jnp.where(dev_iota == d, block, 0.0), axis=0, keepdims=True)

    def columns(rows):
        rows = rows + [jnp.zeros((128 - len(rows), 128), F32)]
        return jnp.concatenate(rows, axis=0).T

    def compute(u):
        for hf in range(2):
            rs = pl.ds(hf * hb, hb)
            ids = row_of(gbuf[u, 1, :, pl.ds(hf * hb, hb)], ep)
            cols = columns([(ids == float(e)).astype(F32) for e in range(e_local)])
            for e in range(e_local):
                keep = jnp.broadcast_to(cols[:, e:e + 1], (hb, 128)).astype(BF16)
                m_scr[e, rs, :] = keep
                for b in range(hidden // 128):
                    xm[rs, e * hidden + b * 128:e * hidden + (b + 1) * 128] = hbuf[u, rs, b * 128:(b + 1) * 128] * keep

        def up_tile(n, carry):
            cs = pl.ds(pl.multiple_of(n * 256, 256), 256)
            a = jnp.dot(xm[...], wg[:, cs], preferred_element_type=F32)
            b = jnp.dot(xm[...], wu[:, cs], preferred_element_type=F32)
            g = (a * (1.0 / (1.0 + jnp.exp(-a))) * b).astype(BF16)
            for e in range(e_local):
                for q in range(2):
                    gm[:, pl.ds(pl.multiple_of(n * 256, 256) + e * ff + q * 128, 128)] = g[:, q * 128:(q + 1) * 128] * m_scr[e]
            return carry

        lax.fori_loop(0, ff // 256, up_tile, 0)

        def down_tile(n, carry):
            cs = pl.ds(pl.multiple_of(n * 256, 256), 256)
            ybuf[u, :, cs] = jnp.dot(gm[...], wd[:, cs], preferred_element_type=F32).astype(BF16)
            return carry

        lax.fori_loop(0, hidden // 256, down_tile, 0)

    def gate_cols(u, lanes, devs):
        blk = gbuf[u, 0, :, lanes]
        return columns([row_of(blk, d) for d in devs])

    def take_gate(u):
        if u == 7:
            gate[1].wait_recv()
            gbuf[7] = gsrc[1]
            return
        rel, hf = ((1, 0), (3, 1), (2, 0), (2, 1), (1, 1), (3, 0))[u - 1]
        for q in range(2):
            if u in (1, 2, 3):
                gate[2 * rel + q].wait_recv()
            gbuf[u, :, :, pl.ds(q * hb, hb)] = gsrc[2 * rel + q, :, :, pl.ds(hf * hb, hb)]

    def send_sums():
        for slot, u in ((0, 5), (1, 6)):
            peer_y[u].wait_recv()
        for p in range(2):
            rows = pl.ds(p * qb, qb)
            for slot, u, ch in ((0, 5, right), (1, 6, left)):
                for co in range(2):
                    piece = y_far.at[slot, co, rows]
                    rcopy(piece, piece, send_f.at[slot, p, co], recv_f.at[slot, co, p], ch, core).wait_recv()
                cols = gate_cols(u, pl.ds(0, 128), [ep, chip * 2 + other, ch * 2, ch * 2 + 1])[p * qb:(p + 1) * qb]
                s_out[slot, rows] = (ybuf[u, rows, :].astype(F32) * cols[:, 0:1] + y_peer[slot, rows].astype(F32) * cols[:, 1:2]
                                     + y_far[slot, 0, rows].astype(F32) * cols[:, 2:3] + y_far[slot, 1, rows].astype(F32) * cols[:, 3:4])
                sums[slot, p].start()

    def before(u):
        if u == 0:
            for c in w_copies:
                c.wait()
        if u == 1:
            for v in (1, 2):
                dispatch[v].wait_recv()
                dispatch[v + 2].start()
                to_peer[v].start()
        if u == 2:
            for v in (5, 6):
                dispatch[v].wait_recv()
                to_peer[v].start()
        if u == 3:
            for v in (3, 4):
                dispatch[v].wait_recv()
                to_peer[v].start()
        if u == 7:
            send_sums()
        if u >= 1:
            to_peer[u].wait_recv()
            take_gate(u)

    def after(u):
        if u in (1, 2):
            for c in near[u]:
                c.start()
        if u in (3, 4):
            for c in far[u]:
                c.start()
        if u in (5, 6, 7):
            peer_y[u].start()

    def unit(u, carry):
        for v in range(8):
            pl.when(u == v)(functools.partial(before, v))
        compute(u)
        for v in range(1, 8):
            pl.when(u == v)(functools.partial(after, v))
        return carry

    lax.fori_loop(0, 8, unit, 0)

    peer_y[7].wait_recv()
    for hf, ch in ((0, right), (1, left)):
        rs = pl.ds(hf * hb, hb)
        for co in range(2):
            rcopy(y_near.at[hf, co], y_near.at[hf, co], send_n.at[hf, co], recv_n.at[hf, co], ch, core).wait_recv()
        cols = gate_cols(0, rs, [ep, chip * 2 + other, ch * 2, ch * 2 + 1])
        acc_scr[rs, :] = x1_ref[rs, :].astype(F32) + (
            ybuf[0, rs, :].astype(F32) * cols[:, 0:1] + y_own[rs, :].astype(F32) * cols[:, 1:2]
            + y_near[hf, 0].astype(F32) * cols[:, 2:3] + y_near[hf, 1].astype(F32) * cols[:, 3:4])
    for p in range(2):
        for hf in range(2):
            rows = pl.ds(p * qb, qb)
            rs = pl.ds(hf * hb + p * qb, qb)
            sums[1 - hf, p].wait_recv()
            out_ref[rs, :] = (acc_scr[rs, :] + s_in[hf, rows]).astype(BF16)

    for group in (list(dispatch.values()), list(gate.values()), list(to_peer.values()), near[1], near[2], far[3], far[4], list(peer_y.values()), list(sums.values())):
        for c in group:
            c.wait_send()


def moe(h2, ri, x1, w_gate, w_up, w_down, ep_size):
    n_tok, hidden = h2.shape
    e_local, _, ff = w_gate.shape
    hb = n_tok // 2
    dma = pltpu.SemaphoreType.DMA
    vmem = pl.BlockSpec(memory_space=pltpu.VMEM)
    hbm = pl.BlockSpec(memory_space=pl.ANY)
    return pl.pallas_call(
        functools.partial(moe_kernel, ep_size // 2),
        out_shape=jax.ShapeDtypeStruct((n_tok, hidden), BF16),
        in_specs=[vmem, vmem, vmem, hbm, hbm, hbm],
        out_specs=vmem,
        scratch_shapes=[
            pltpu.VMEM((e_local * hidden, ff), BF16), pltpu.VMEM((e_local * hidden, ff), BF16), pltpu.VMEM((e_local * ff, hidden), BF16),
            pltpu.VMEM((8, n_tok, hidden), BF16), pltpu.VMEM((8, 2, ep_size, n_tok), F32), pltpu.VMEM((8, 2, ep_size, n_tok), F32),
            pltpu.VMEM((n_tok, e_local * hidden), BF16), pltpu.VMEM((n_tok, e_local * ff), BF16), pltpu.VMEM((e_local, n_tok, 128), BF16),
            pltpu.VMEM((8, n_tok, hidden), BF16), pltpu.VMEM((2, 2, hb, hidden), BF16), pltpu.VMEM((2, 2, hb, hidden), BF16), pltpu.VMEM((2, hb, hidden), BF16), pltpu.VMEM((n_tok, hidden), BF16),
            pltpu.VMEM((2, hb, hidden), F32), pltpu.VMEM((2, hb, hidden), F32), pltpu.VMEM((n_tok, hidden), F32),
            dma((3,)), dma((8,)), dma((8,)), dma((8,)), dma((8,)), dma((8,)), dma((8,)), dma((2, 2)), dma((2, 2)), dma((2, 2, 2)), dma((2, 2, 2)), dma((3,)), dma((3,)), dma((2, 2)), dma((2, 2)),
        ],
        compiler_params=pltpu.CompilerParams(collective_id=0, has_side_effects=True),
        name="moe",
    )(h2, ri, x1, w_gate.reshape(e_local * hidden, ff), w_up.reshape(e_local * hidden, ff), w_down.reshape(e_local * ff, hidden))


def solution(mesh):
    ep_size = mesh.shape['ep']
    row_spec = P(('dp', 'ep'))
    replicated = P()
    expert_spec = P('ep')
    in_specs = (row_spec,) * 5 + (replicated,) * 9 + (expert_spec,) * 3

    def device_step(x_in, k_cache, v_cache, cache_len, topk_idx, ln_attn, w_q, w_k, w_v, q_norm, k_norm, w_o, ln_moe, w_router, w_gate, w_up, w_down):
        x1, h2, ri, k_new, v_new = attention(x_in, k_cache, v_cache, cache_len, topk_idx, ln_attn, w_q, w_k, w_v, q_norm, k_norm, w_o, ln_moe, w_router, ep_size)
        return moe(h2, ri, x1, w_gate, w_up, w_down, ep_size), k_new, v_new

    return jax.shard_map(device_step, mesh=mesh, in_specs=in_specs, out_specs=(row_spec,) * 3, check_vma=False)
```

time: 101 us -> 85.8 us (0.85)
  Pallas kernels: 95.3 us -> 82.8 us
  local copies, waits for them, and re-layouts: 4.42 us -> 1.87 us
    pallas_call x1, Pallas kernels: 24.9 us -> 18.4 us  [attention(): pl.pallas_call(attn_kernel, in_specs=[vmem] * 9 + [hbm] * 6, out_specs=[v...]
    pallas_call x1, Pallas kernels: 70.4 us -> 64.4 us  [moe(): pl.pallas_call(functools.partial(moe_kernel, ep_size // 2), out_shape=jax...]
    reshape x2 -> x0, local copies, waits for them, and re-layouts: 2.55 us -> none  [the longest x1 1.28 us: attention(): ln_moe.reshape(1, hidden)]
where the time goes in v2:
time: 85.8 us; the launch traced here: 85.3 us
  Pallas kernels  82.8 us (97%)
  local copies, waits for them, and re-layouts  1.87 us (2%)
    pallas_call x1, Pallas kernels, moe(): pl.pallas_call(functools.partial(moe_kernel, ep_size // 2), out_shape=jax...  64.4 us
    pallas_call x1, Pallas kernels, attention(): pl.pallas_call(attn_kernel, in_specs=[vmem] * 9 + [hbm] * 6, out_specs=[v...  18.4 us
    unnamed x1, local copies, waits for them, and re-layouts  1.87 us

profile of v2, /device:TPU:81, one launch (start us, length us, event | category | flops | bytes accessed | tf_op | source)
XLA Modules:
  0.0 85.3 jit_solution(3344777504859671151)
XLA Ops:
  0.6 18.4 %attend.1 = (bf16[256,1024]{1,0:T(8,128)(2,1)}, bf16[256,1024]{1,0:T(8,128)(2,1)}, f32[2,8,256]{2,1,0:T(8,128)}, bf16[32,8,64,256]{3,2,1,0:T(8,128)(2,1)}, bf16[32,8,64,256]{3,2,1,0:T(8,128)(2,1)}) custom-call(f32[32,128]{1,0:T(8,128)} %constant.2.clone.freq_ref, bf16[256,1024]{1,0:T(8,128)(2,1)} %x_ref.1, s32[1,256]{1,0:T(1,128)} %bitcast.19, ...), custom_call_target="tpu_custom_call" | custom-call | tf_op jit(solution)/shard_map/attend/pallas_call | solution.py:217
  19.0 64.4 %moe.1 = bf16[256,1024]{1,0:T(8,128)(2,1)} custom-call(bf16[256,1024]{1,0:T(8,128)(2,1)} %get-tuple-element.8.h2_ref, f32[2,8,256]{2,1,0:T(8,128)} %get-tuple-element.9.ri_ref, bf16[256,1024]{1,0:T(8,128)(2,1)} %get-tuple-element.10.x1_ref, bf16[4096,512]{1,0:T(8,128)(2,1)} %bitcast.14, bf16[4096,512]{1,0:T(8,128)(2,1)} %bitcast.15, bf16[2048,1024]{1,0:T(8,128)(2,1)} %bitcast.16), custom_call_target="tpu_custom_call" | custom-call | tf_op jit(solution)/shard_map/moe/pallas_call | solution.py:460
  83.5 1.9 %copy.22 = bf16[256,1024]{1,0:T(8,128)(2,1)} copy(bf16[256,1024]{1,0:T(8,128)(2,1)} %moe.1) | data formatting | bytes 1048576

commit v3 on v2

--- a/solution.py
+++ b/solution.py
@@ -23,7 +23,7 @@
     return parts[0]
 
 
-def attn_kernel(freq_ref, x_ref, len_ref, topk_ref, lna_ref, qn_ref, kn_ref, lnm_ref, wr_ref, wq_hbm, wk_hbm, wv_hbm, wo_hbm, kc_hbm, vc_hbm,
+def attn_body(small_copies, freq_ref, x_ref, len_ref, topk_ref, lna_ref, qn_ref, kn_ref, lnm_ref, wr_ref, wq_hbm, wk_hbm, wv_hbm, wo_hbm, kc_hbm, vc_hbm,
                 x1_ref, h2_ref, ri_ref, kco_hbm, vco_hbm,
                 wq_scr, wk_scr, wv_scr, wo_scr, kbuf, vbuf, h_scr, cos_scr, sin_scr, qg_scr, kg_scr, len_scr, q_scr, kn_scr, vn_scr, s_scr, o_scr,
                 w_sem, kin_sem, vin_sem, kout_sem, vout_sem):
@@ -42,11 +42,13 @@
     def writes(g):
         return (pltpu.make_async_copy(kbuf.at[g], kco_hbm.at[:, g], kout_sem.at[g]), pltpu.make_async_copy(vbuf.at[g], vco_hbm.at[:, g], vout_sem.at[g]))
 
-    for c in w_copies[:3]:
+    for c in small_copies + w_copies[:3]:
         c.start()
     for g in range(early):
         for c in reads(g):
             c.start()
+    for c in small_copies:
+        c.wait()
 
     xf = x_ref[...].astype(F32)
     ms = jnp.mean(xf * xf, axis=1, keepdims=True)
@@ -204,6 +206,17 @@
     lax.fori_loop(0, n_head, drain, 0)
 
 
+def attn_kernel(n_small, *refs):
+    small, rest = refs[:n_small], refs[n_small:]
+    held, sem = rest[-n_small - 1:-1], rest[-1]
+    copies = [pltpu.make_async_copy(src, dst, sem.at[i]) for i, (src, dst) in enumerate(zip(small, held))]
+    attn_body(copies, *held, *rest[:-n_small - 1])
+
+
+def in_hbm(arrays):
+    return [pltpu.with_memory_space_constraint(a, pltpu.HBM) for a in arrays]
+
+
 def attention(x_in, k_cache, v_cache, cache_len, topk_idx, ln_attn, w_q, w_k, w_v, q_norm, k_norm, w_o, ln_moe, w_router, ep_size):
     n_tok, hidden = x_in.shape
     _, n_slots, kv_heads, head_dim = k_cache.shape
@@ -212,11 +225,12 @@
     kt = k_cache.transpose(1, 2, 3, 0)
     vt = v_cache.transpose(1, 2, 3, 0)
     vmem = pl.BlockSpec(memory_space=pltpu.VMEM)
-    hbm = pl.BlockSpec(memory_space=pl.ANY)
+    hbm = pl.BlockSpec(memory_space=pltpu.HBM)
     dma = pltpu.SemaphoreType.DMA
+    small = [freq, x_in, cache_len.reshape(1, n_tok), topk_idx.T, ln_attn, q_norm.reshape(1, head_dim), k_norm.reshape(1, head_dim), ln_moe, w_router.T]
     out = pl.pallas_call(
-        attn_kernel,
-        in_specs=[vmem] * 9 + [hbm] * 6,
+        functools.partial(attn_kernel, len(small)),
+        in_specs=[hbm] * (len(small) + 6),
         out_specs=[vmem, vmem, vmem, hbm, hbm],
         out_shape=[
             jax.ShapeDtypeStruct((n_tok, hidden), BF16), jax.ShapeDtypeStruct((n_tok, hidden), BF16), jax.ShapeDtypeStruct((2, ep_size, n_tok), F32),
@@ -230,10 +244,10 @@
             pltpu.VMEM((2 * kv_heads, head_dim, n_tok), F32), pltpu.VMEM((kv_heads, head_dim, n_tok), BF16), pltpu.VMEM((kv_heads, head_dim, n_tok), BF16),
             pltpu.VMEM((2, n_slots, n_tok), F32), pltpu.VMEM((n_tok, w_q.shape[1]), BF16),
             dma((4,)), dma((kv_heads,)), dma((kv_heads,)), dma((kv_heads,)), dma((kv_heads,)),
-        ],
+        ] + [pltpu.VMEM(a.shape, a.dtype) for a in small] + [dma((len(small),))],
+        compiler_params=pltpu.CompilerParams(vmem_limit_bytes=40 << 20),
         name="attend",
-    )(freq, x_in, cache_len.reshape(1, n_tok), topk_idx.T, ln_attn, q_norm.reshape(1, head_dim), k_norm.reshape(1, head_dim),
-      ln_moe, w_router.T, w_q, w_k, w_v, w_o, kt, vt)
+    )(*in_hbm(small + [w_q, w_k, w_v, w_o, kt, vt]))
     x1, h2, ri, kto, vto = out
     return x1, h2, ri, kto.transpose(3, 0, 1, 2), vto.transpose(3, 0, 1, 2)
 
@@ -301,11 +315,11 @@
         sums[0, p] = rcopy(s_out.at[0, rows], s_in.at[1, rows], send_s.at[0, p], recv_s.at[1, p], left, core)
         sums[1, p] = rcopy(s_out.at[1, rows], s_in.at[0, rows], send_s.at[1, p], recv_s.at[0, p], right, core)
 
-    for c in w_copies:
-        c.start()
     barrier = pltpu.get_barrier_semaphore()
     for d in range(1, 2 * n_chip):
         pl.semaphore_signal(barrier, inc=1, device_id={"ep": lax.rem(ep + d, 2 * n_chip)}, device_id_type=MESH)
+    for c in w_copies:
+        c.start()
     pl.semaphore_wait(barrier, 2 * n_chip - 1)
 
     dispatch[1].start()
@@ -327,32 +341,38 @@
         rows = rows + [jnp.zeros((128 - len(rows), 128), F32)]
         return jnp.concatenate(rows, axis=0).T
 
-    def compute(u):
-        for hf in range(2):
+    def compute(u, count):
+        n_rows = count * n_tok
+        for hf in range(2 * count):
+            v = u + hf // 2
+            src = pl.ds((hf % 2) * hb, hb)
             rs = pl.ds(hf * hb, hb)
-            ids = row_of(gbuf[u, 1, :, pl.ds(hf * hb, hb)], ep)
+            ids = row_of(gbuf[v, 1, :, src], ep)
             cols = columns([(ids == float(e)).astype(F32) for e in range(e_local)])
             for e in range(e_local):
                 keep = jnp.broadcast_to(cols[:, e:e + 1], (hb, 128)).astype(BF16)
                 m_scr[e, rs, :] = keep
                 for b in range(hidden // 128):
-                    xm[rs, e * hidden + b * 128:e * hidden + (b + 1) * 128] = hbuf[u, rs, b * 128:(b + 1) * 128] * keep
+                    xm[rs, e * hidden + b * 128:e * hidden + (b + 1) * 128] = hbuf[v, src, b * 128:(b + 1) * 128] * keep
+        rows = pl.ds(0, n_rows)
 
         def up_tile(n, carry):
             cs = pl.ds(pl.multiple_of(n * 256, 256), 256)
-            a = jnp.dot(xm[...], wg[:, cs], preferred_element_type=F32)
-            b = jnp.dot(xm[...], wu[:, cs], preferred_element_type=F32)
+            a = jnp.dot(xm[rows], wg[:, cs], preferred_element_type=F32)
+            b = jnp.dot(xm[rows], wu[:, cs], preferred_element_type=F32)
             g = (a * (1.0 / (1.0 + jnp.exp(-a))) * b).astype(BF16)
             for e in range(e_local):
                 for q in range(2):
-                    gm[:, pl.ds(pl.multiple_of(n * 256, 256) + e * ff + q * 128, 128)] = g[:, q * 128:(q + 1) * 128] * m_scr[e]
+                    gm[rows, pl.ds(pl.multiple_of(n * 256, 256) + e * ff + q * 128, 128)] = g[:, q * 128:(q + 1) * 128] * m_scr[e, rows]
             return carry
 
         lax.fori_loop(0, ff // 256, up_tile, 0)
 
         def down_tile(n, carry):
             cs = pl.ds(pl.multiple_of(n * 256, 256), 256)
-            ybuf[u, :, cs] = jnp.dot(gm[...], wd[:, cs], preferred_element_type=F32).astype(BF16)
+            y = jnp.dot(gm[rows], wd[:, cs], preferred_element_type=F32).astype(BF16)
+            for i in range(count):
+                ybuf[u + i, :, cs] = y[i * n_tok:(i + 1) * n_tok]
             return carry
 
         lax.fori_loop(0, hidden // 256, down_tile, 0)
@@ -395,12 +415,8 @@
                 dispatch[v].wait_recv()
                 dispatch[v + 2].start()
                 to_peer[v].start()
-        if u == 2:
-            for v in (5, 6):
-                dispatch[v].wait_recv()
-                to_peer[v].start()
         if u == 3:
-            for v in (3, 4):
+            for v in (5, 6, 3, 4):
                 dispatch[v].wait_recv()
                 to_peer[v].start()
         if u == 7:
@@ -419,15 +435,31 @@
         if u in (5, 6, 7):
             peer_y[u].start()
 
-    def unit(u, carry):
-        for v in range(8):
-            pl.when(u == v)(functools.partial(before, v))
-        compute(u)
-        for v in range(1, 8):
-            pl.when(u == v)(functools.partial(after, v))
+    rounds = ((0,), (1, 2), (3, 4), (5, 6), (7,))
+
+    def unit_round(r, carry):
+        for v, units in enumerate(rounds):
+            @pl.when(r == v)
+            def _():
+                for u in units:
+                    before(u)
+
+        @pl.when(lax.rem(r, 4) == 0)
+        def _():
+            compute((r // 4) * 7, 1)
+
+        @pl.when(lax.rem(r, 4) != 0)
+        def _():
+            compute(2 * r - 1, 2)
+
+        for v, units in enumerate(rounds):
+            @pl.when(r == v)
+            def _():
+                for u in units:
+                    after(u)
         return carry
 
-    lax.fori_loop(0, 8, unit, 0)
+    lax.fori_loop(0, len(rounds), unit_round, 0)
 
     peer_y[7].wait_recv()
     for hf, ch in ((0, right), (1, left)):
@@ -456,23 +488,23 @@
     hb = n_tok // 2
     dma = pltpu.SemaphoreType.DMA
     vmem = pl.BlockSpec(memory_space=pltpu.VMEM)
-    hbm = pl.BlockSpec(memory_space=pl.ANY)
+    hbm = pl.BlockSpec(memory_space=pltpu.HBM)
     return pl.pallas_call(
         functools.partial(moe_kernel, ep_size // 2),
         out_shape=jax.ShapeDtypeStruct((n_tok, hidden), BF16),
-        in_specs=[vmem, vmem, vmem, hbm, hbm, hbm],
+        in_specs=[vmem] * 3 + [hbm] * 3,
         out_specs=vmem,
         scratch_shapes=[
             pltpu.VMEM((e_local * hidden, ff), BF16), pltpu.VMEM((e_local * hidden, ff), BF16), pltpu.VMEM((e_local * ff, hidden), BF16),
             pltpu.VMEM((8, n_tok, hidden), BF16), pltpu.VMEM((8, 2, ep_size, n_tok), F32), pltpu.VMEM((8, 2, ep_size, n_tok), F32),
-            pltpu.VMEM((n_tok, e_local * hidden), BF16), pltpu.VMEM((n_tok, e_local * ff), BF16), pltpu.VMEM((e_local, n_tok, 128), BF16),
+            pltpu.VMEM((2 * n_tok, e_local * hidden), BF16), pltpu.VMEM((2 * n_tok, e_local * ff), BF16), pltpu.VMEM((e_local, 2 * n_tok, 128), BF16),
             pltpu.VMEM((8, n_tok, hidden), BF16), pltpu.VMEM((2, 2, hb, hidden), BF16), pltpu.VMEM((2, 2, hb, hidden), BF16), pltpu.VMEM((2, hb, hidden), BF16), pltpu.VMEM((n_tok, hidden), BF16),
             pltpu.VMEM((2, hb, hidden), F32), pltpu.VMEM((2, hb, hidden), F32), pltpu.VMEM((n_tok, hidden), F32),
             dma((3,)), dma((8,)), dma((8,)), dma((8,)), dma((8,)), dma((8,)), dma((8,)), dma((2, 2)), dma((2, 2)), dma((2, 2, 2)), dma((2, 2, 2)), dma((3,)), dma((3,)), dma((2, 2)), dma((2, 2)),
         ],
-        compiler_params=pltpu.CompilerParams(collective_id=0, has_side_effects=True),
+        compiler_params=pltpu.CompilerParams(collective_id=0, has_side_effects=True, vmem_limit_bytes=46 << 20),
         name="moe",
-    )(h2, ri, x1, w_gate.reshape(e_local * hidden, ff), w_up.reshape(e_local * hidden, ff), w_down.reshape(e_local * ff, hidden))
+    )(h2, ri, x1, *in_hbm([w_gate.reshape(e_local * hidden, ff), w_up.reshape(e_local * hidden, ff), w_down.reshape(e_local * ff, hidden)]))
 
 
 def solution(mesh):

time: 85.8 us -> 80.3 us (0.936)
  Pallas kernels: 82.8 us -> 78.7 us
  local copies, waits for them, and re-layouts: 1.87 us -> 0.8 us
    pallas_call x1, Pallas kernels: 64.4 us -> 62 us  [moe(): pl.pallas_call(functools.partial(moe_kernel, ep_size // 2), out_shape=jax...]
    pallas_call x1, Pallas kernels: 18.4 us -> 16.7 us  [attention(): pl.pallas_call(functools.partial(attn_kernel, len(small)), in_specs=[hbm]...]
    unnamed x1, local copies, waits for them, and re-layouts: 1.87 us -> 0.8 us
where the time goes in v3:
time: 80.3 us; the launch traced here: 80.2 us
  Pallas kernels  78.7 us (98%)
    pallas_call x1, Pallas kernels, moe(): pl.pallas_call(functools.partial(moe_kernel, ep_size // 2), out_shape=jax...  62 us
    pallas_call x1, Pallas kernels, attention(): pl.pallas_call(functools.partial(attn_kernel, len(small)), in_specs=[hbm]...  16.7 us

profile of v3, /device:TPU:81, one launch (start us, length us, event | category | flops | bytes accessed | tf_op | source)
XLA Modules:
  0.0 80.2 jit_solution(3918547964395106795)
XLA Ops:
  0.6 16.7 %attend.1 = (bf16[256,1024]{1,0:T(8,128)(2,1)S(1)}, bf16[256,1024]{1,0:T(8,128)(2,1)S(1)}, f32[2,8,256]{2,1,0:T(8,128)S(1)}, bf16[32,8,64,256]{3,2,1,0:T(8,128)(2,1)}, bf16[32,8,64,256]{3,2,1,0:T(8,128)(2,1)}) custom-call(f32[32,128]{1,0:T(8,128)} %constant.2.clone.refs_0_, bf16[256,1024]{1,0:T(8,128)(2,1)} %refs_1_.1, s32[1,256]{1,0:T(1,128)} %bitcast.19, ...), custom_call_target="tpu_custom_call" | custom-call | tf_op jit(solution)/shard_map/attend/pallas_call | solution.py:231
  17.3 62.0 %moe.1 = bf16[256,1024]{1,0:T(8,128)(2,1)S(1)} custom-call(bf16[256,1024]{1,0:T(8,128)(2,1)S(1)} %get-tuple-element.8.h2_ref, f32[2,8,256]{2,1,0:T(8,128)S(1)} %get-tuple-element.9.ri_ref, bf16[256,1024]{1,0:T(8,128)(2,1)S(1)} %get-tuple-element.10.x1_ref, bf16[4096,512]{1,0:T(8,128)(2,1)} %bitcast.14, bf16[4096,512]{1,0:T(8,128)(2,1)} %bitcast.15, ...), custom_call_target="tpu_custom_call" | custom-call | tf_op jit(solution)/shard_map/moe/pallas_call | solution.py:492
  79.4 0.8 copy.22

commit v4 on v3

--- a/solution.py
+++ b/solution.py
@@ -132,7 +132,7 @@
                     s_scr[j, pl.ds(pl.multiple_of(i * 8, 8), 8), lanes] = sublane_sums(parts[j])
                 return carry
 
-            lax.fori_loop(0, n_slots // 8, score_block, 0)
+            lax.fori_loop(0, n_slots // 8, score_block, 0, unroll=2)
             slot = lax.broadcasted_iota(jnp.int32, (n_slots, 128), 0)
             len_row = len_ref[:, lanes]
             kn = kn_scr[g, :, lanes].astype(F32)
@@ -161,7 +161,7 @@
                             accs[j][r] = accs[j][r] + prob[j][si:si + 1] * vf
                 return tuple(jnp.concatenate(a, axis=0) for a in accs)
 
-            accs = lax.fori_loop(0, n_slots // 8, value_block, tuple(accs))
+            accs = lax.fori_loop(0, n_slots // 8, value_block, tuple(accs), unroll=2)
             o_scr[pl.ds(lt * 128, 128), pl.ds(pl.multiple_of(g * 128, 128), 128)] = jnp.concatenate(accs, axis=0).T.astype(BF16)
         for c in writes(g):
             c.start()
@@ -277,16 +277,16 @@
     top = pl.ds(0, hb)
     bot = pl.ds(hb, hb)
 
-    w_copies = [pltpu.make_async_copy(wg_hbm, wg, w_sem.at[0]), pltpu.make_async_copy(wu_hbm, wu, w_sem.at[1]), pltpu.make_async_copy(wd_hbm, wd, w_sem.at[2])]
-
-    dispatch = {
-        1: rcopy(h2_ref.at[top], hbuf.at[1, top], send_h.at[1], recv_h.at[1], right, core),
-        2: rcopy(h2_ref.at[bot], hbuf.at[2, top], send_h.at[2], recv_h.at[2], left, core),
-        5: rcopy(h2_ref.at[bot], hbuf.at[5, top], send_h.at[5], recv_h.at[5], right, core),
-        6: rcopy(h2_ref.at[top], hbuf.at[6, top], send_h.at[6], recv_h.at[6], left, core),
-        3: rcopy(hbuf.at[1, top], hbuf.at[3, top], send_h.at[3], recv_h.at[3], right, core),
-        4: rcopy(hbuf.at[2, top], hbuf.at[4, top], send_h.at[4], recv_h.at[4], left, core),
-    }
+    w_copies = [pltpu.make_async_copy(src, dst, w_sem.at[i]) for i, (src, dst) in enumerate(((wg_hbm, wg), (wu_hbm, wu), (wd_hbm, wd)))]
+
+    q0 = pl.ds(0, qb)
+    q1 = pl.ds(qb, qb)
+    dispatch = {}
+    for key, u, src, rows, ch in (
+        (1, 1, h2_ref.at[top], top, right), (2, 2, h2_ref.at[bot], top, left), (3, 3, hbuf.at[1, top], top, right), (4, 4, hbuf.at[2, top], top, left),
+        (5, 5, h2_ref.at[pl.ds(hb, qb)], q0, right), (6, 6, h2_ref.at[q0], q0, left), (0, 5, h2_ref.at[pl.ds(hb + qb, qb)], q1, right), (7, 6, h2_ref.at[q1], q1, left),
+    ):
+        dispatch[key] = rcopy(src, hbuf.at[u, rows], send_h.at[key], recv_h.at[key], ch, core)
     to_peer = {u: rcopy(hbuf.at[u, top], hbuf.at[u, bot], send_p.at[u], recv_p.at[u], chip, other) for u in range(1, 7)}
     to_peer[7] = rcopy(h2_ref, hbuf.at[7], send_p.at[7], recv_p.at[7], chip, other)
     gate = {}
@@ -306,9 +306,8 @@
             rows = pl.ds(p * qb, qb)
             far[u].append(rcopy(ybuf.at[u, rows], y_far.at[slot, core, rows], send_f.at[slot, p, 0], recv_f.at[slot, core, p], ch, core))
             far[u].append(rcopy(ybuf.at[u, pl.ds(hb + p * qb, qb)], y_far.at[slot, core, rows], send_f.at[slot, p, 1], recv_f.at[slot, core, p], ch, other))
-    peer_y = {5: rcopy(ybuf.at[5, bot], y_peer.at[0], send_y.at[0], recv_y.at[0], chip, other),
-              6: rcopy(ybuf.at[6, bot], y_peer.at[1], send_y.at[1], recv_y.at[1], chip, other),
-              7: rcopy(ybuf.at[7], y_own, send_y.at[2], recv_y.at[2], chip, other)}
+    peer_y = {u: rcopy(ybuf.at[u, bot], y_peer.at[i], send_y.at[i], recv_y.at[i], chip, other) for i, u in enumerate((5, 6))}
+    peer_y[7] = rcopy(ybuf.at[7], y_own, send_y.at[2], recv_y.at[2], chip, other)
     sums = {}
     for p in range(2):
         rows = pl.ds(p * qb, qb)
@@ -379,7 +378,8 @@
 
     def gate_cols(u, lanes, devs):
         blk = gbuf[u, 0, :, lanes]
-        return columns([row_of(blk, d) for d in devs])
+        cols = columns([row_of(blk, d) for d in devs])
+        return [cols[:, i:i + 1] for i in range(len(devs))]
 
     def take_gate(u):
         if u == 7:
@@ -401,9 +401,9 @@
                 for co in range(2):
                     piece = y_far.at[slot, co, rows]
                     rcopy(piece, piece, send_f.at[slot, p, co], recv_f.at[slot, co, p], ch, core).wait_recv()
-                cols = gate_cols(u, pl.ds(0, 128), [ep, chip * 2 + other, ch * 2, ch * 2 + 1])[p * qb:(p + 1) * qb]
-                s_out[slot, rows] = (ybuf[u, rows, :].astype(F32) * cols[:, 0:1] + y_peer[slot, rows].astype(F32) * cols[:, 1:2]
-                                     + y_far[slot, 0, rows].astype(F32) * cols[:, 2:3] + y_far[slot, 1, rows].astype(F32) * cols[:, 3:4])
+                c_own, c_peer, c_a, c_b = [c[p * qb:(p + 1) * qb] for c in gate_cols(u, top, [ep, chip * 2 + other, ch * 2, ch * 2 + 1])]
+                s_out[slot, rows] = (ybuf[u, rows, :].astype(F32) * c_own + y_peer[slot, rows].astype(F32) * c_peer
+                                     + y_far[slot, 0, rows].astype(F32) * c_a + y_far[slot, 1, rows].astype(F32) * c_b)
                 sums[slot, p].start()
 
     def before(u):
@@ -415,9 +415,16 @@
                 dispatch[v].wait_recv()
                 dispatch[v + 2].start()
                 to_peer[v].start()
+            dispatch[0].start()
+            dispatch[7].start()
         if u == 3:
-            for v in (5, 6, 3, 4):
+            for v in (3, 4):
                 dispatch[v].wait_recv()
+                to_peer[v].start()
+        if u == 5:
+            for v, w in ((5, 0), (6, 7)):
+                dispatch[v].wait_recv()
+                dispatch[w].wait_recv()
                 to_peer[v].start()
         if u == 7:
             send_sums()
@@ -466,10 +473,10 @@
         rs = pl.ds(hf * hb, hb)
         for co in range(2):
             rcopy(y_near.at[hf, co], y_near.at[hf, co], send_n.at[hf, co], recv_n.at[hf, co], ch, core).wait_recv()
-        cols = gate_cols(0, rs, [ep, chip * 2 + other, ch * 2, ch * 2 + 1])
+        c_own, c_peer, c_a, c_b = gate_cols(0, rs, [ep, chip * 2 + other, ch * 2, ch * 2 + 1])
         acc_scr[rs, :] = x1_ref[rs, :].astype(F32) + (
-            ybuf[0, rs, :].astype(F32) * cols[:, 0:1] + y_own[rs, :].astype(F32) * cols[:, 1:2]
-            + y_near[hf, 0].astype(F32) * cols[:, 2:3] + y_near[hf, 1].astype(F32) * cols[:, 3:4])
+            ybuf[0, rs, :].astype(F32) * c_own + y_own[rs, :].astype(F32) * c_peer
+            + y_near[hf, 0].astype(F32) * c_a + y_near[hf, 1].astype(F32) * c_b)
     for p in range(2):
         for hf in range(2):
             rows = pl.ds(p * qb, qb)
@@ -500,8 +507,8 @@
             pltpu.VMEM((2 * n_tok, e_local * hidden), BF16), pltpu.VMEM((2 * n_tok, e_local * ff), BF16), pltpu.VMEM((e_local, 2 * n_tok, 128), BF16),
             pltpu.VMEM((8, n_tok, hidden), BF16), pltpu.VMEM((2, 2, hb, hidden), BF16), pltpu.VMEM((2, 2, hb, hidden), BF16), pltpu.VMEM((2, hb, hidden), BF16), pltpu.VMEM((n_tok, hidden), BF16),
             pltpu.VMEM((2, hb, hidden), F32), pltpu.VMEM((2, hb, hidden), F32), pltpu.VMEM((n_tok, hidden), F32),
-            dma((3,)), dma((8,)), dma((8,)), dma((8,)), dma((8,)), dma((8,)), dma((8,)), dma((2, 2)), dma((2, 2)), dma((2, 2, 2)), dma((2, 2, 2)), dma((3,)), dma((3,)), dma((2, 2)), dma((2, 2)),
-        ],
+            dma((3,)),
+        ] + [dma((8,))] * 6 + [dma((2, 2))] * 2 + [dma((2, 2, 2))] * 2 + [dma((3,))] * 2 + [dma((2, 2))] * 2,
         compiler_params=pltpu.CompilerParams(collective_id=0, has_side_effects=True, vmem_limit_bytes=46 << 20),
         name="moe",
     )(h2, ri, x1, *in_hbm([w_gate.reshape(e_local * hidden, ff), w_up.reshape(e_local * hidden, ff), w_down.reshape(e_local * ff, hidden)]))

time: 80.3 us -> 79.4 us (0.989)
  Pallas kernels: 78.7 us -> 77.6 us
where the time goes in v4:
time: 79.4 us; the launch traced here: 79.1 us
  Pallas kernels  77.6 us (98%)
  local copies, waits for them, and re-layouts  0.8 us (1%)
    pallas_call x1, Pallas kernels, moe(): pl.pallas_call(functools.partial(moe_kernel, ep_size // 2), out_shape=jax...  61.3 us
    pallas_call x1, Pallas kernels, attention(): pl.pallas_call(functools.partial(attn_kernel, len(small)), in_specs=[hbm]...  16.4 us

profile of v4, /device:TPU:81, one launch (start us, length us, event | category | flops | bytes accessed | tf_op | source)
XLA Modules:
  0.0 79.1 jit_solution(12670455957282146560)
XLA Ops:
  0.6 16.4 %attend.1 = (bf16[256,1024]{1,0:T(8,128)(2,1)S(1)}, bf16[256,1024]{1,0:T(8,128)(2,1)S(1)}, f32[2,8,256]{2,1,0:T(8,128)S(1)}, bf16[32,8,64,256]{3,2,1,0:T(8,128)(2,1)}, bf16[32,8,64,256]{3,2,1,0:T(8,128)(2,1)}) custom-call(f32[32,128]{1,0:T(8,128)} %constant.2.clone.refs_0_, bf16[256,1024]{1,0:T(8,128)(2,1)} %refs_1_.1, s32[1,256]{1,0:T(1,128)} %bitcast.19, ...), custom_call_target="tpu_custom_call" | custom-call | tf_op jit(solution)/shard_map/attend/pallas_call | solution.py:231
  17.0 61.3 %moe.1 = bf16[256,1024]{1,0:T(8,128)(2,1)S(1)} custom-call(bf16[256,1024]{1,0:T(8,128)(2,1)S(1)} %get-tuple-element.8.h2_ref, f32[2,8,256]{2,1,0:T(8,128)S(1)} %get-tuple-element.9.ri_ref, bf16[256,1024]{1,0:T(8,128)(2,1)S(1)} %get-tuple-element.10.x1_ref, bf16[4096,512]{1,0:T(8,128)(2,1)} %bitcast.14, bf16[4096,512]{1,0:T(8,128)(2,1)} %bitcast.15, ...), custom_call_target="tpu_custom_call" | custom-call | tf_op jit(solution)/shard_map/moe/pallas_call | solution.py:499
  78.3 0.8 %copy.22 = bf16[256,1024]{1,0:T(8,128)(2,1)} copy(bf16[256,1024]{1,0:T(8,128)(2,1)S(1)} %moe.1) | data formatting | bytes 1048576
